TPU v7x, 32 devices: a whole 2x2x4 slice. The times are simulated.
32 devices in a mesh: groups: 2 (over x), owner: 16 (over z, y, core).
Axes of the slice: x: 2, y: 2, z: 4, core: 2. Of those that a mesh axis runs over, the one named last changes fastest.
Arguments:
- queries: bfloat16 [2048, 1024], P(('groups', 'owner')), parts along dimension 0, may hold values from -0.3984375 to 0.3984375
- probes: int32 [2048, 8], P(('groups', 'owner')), parts along dimension 0, may hold values from 0 to 255, as said below
- passages: bfloat16 [256, 256, 1024], P('owner'), may hold values from -6 to 6
- centroids: bfloat16 [256, 1024], P('owner'), may hold values from -6 to 6
- counts: int32 [256], P('owner'), may hold values from 1 to 256
Outputs:
- scores: float32 [2048, 8, 256], P(('groups', 'owner')), parts along dimension 0
- visits: int32 [2048], P(('groups', 'owner')), parts along dimension 0
There are 2 independent parts, one for each index of `groups`. A program takes and returns all parts, laid end to end along the dimension named above; an argument that names none is the same for every part. Nothing has to cross between parts.
Inputs may be any that keep to these rules, and one draw needn't show every extreme that they name: Cluster c belongs to owner index c // 16. In each aligned block of 64 queries (the queries of one index of owner) at most 64 probes name clusters of one owner, and in every draw some owners receive exactly 64 probes from every block. A query may name a cluster more than once.
All inputs are finite; a program needn't handle non-finite values.
Results may differ from a plain program's by a relative error of at most 0.0003.
Values may be sent and summed in bfloat16 or wider, within the bound.
A program may use at most 64 MiB of HBM per device.

v0:
```python
import jax
import jax.numpy as jnp
from jax import lax
from jax.experimental import pallas as pl
from jax.experimental.pallas import tpu as pltpu
from jax.sharding import PartitionSpec as P


def routed_body(queries, probes, passages, centroids, counts):
    owner_count = lax.axis_size("owner")
    per_device, probe_count = probes.shape
    local_count, block_span, feature_width = passages.shape
    capacity = 2 * per_device * probe_count // owner_count
    pair_count = per_device * probe_count
    passage_blocks = jnp.transpose(passages, (0, 2, 1))
    flat_probes = probes.reshape(-1)
    target_owner = flat_probes // local_count
    target_local = flat_probes % local_count
    owner_hits = (
        target_owner[:, None] == jnp.arange(owner_count, dtype=jnp.int32)[None, :]
    ).astype(jnp.int32)
    slot_rank = jnp.sum((jnp.cumsum(owner_hits, axis=0) - owner_hits) * owner_hits, axis=1)
    slot_index = target_owner * capacity + slot_rank
    pair_ids = jnp.arange(pair_count, dtype=jnp.int32)
    slot_match = slot_index[None, :] == jnp.arange(owner_count * capacity, dtype=jnp.int32)[:, None]
    slot_filled = jnp.any(slot_match, axis=1)
    source_pair = jnp.sum(jnp.where(slot_match, pair_ids[None, :], 0), axis=1)
    send_rows = jnp.where(
        slot_filled[:, None], queries[source_pair // probe_count], jnp.zeros((), jnp.bfloat16)
    )
    send_ids = jnp.where(slot_filled, target_local[source_pair], -1)
    query_rows = lax.all_to_all(
        send_rows.reshape(owner_count, capacity, feature_width),
        "owner",
        split_axis=0,
        concat_axis=0,
        tiled=True,
    )
    cluster_ids = lax.all_to_all(
        send_ids.reshape(owner_count, capacity), "owner", split_axis=0, concat_axis=0, tiled=True
    )
    source_count, slot_count = cluster_ids.shape
    row_total = source_count * slot_count
    flat_rows = query_rows.reshape(row_total, feature_width)
    flat_ids = cluster_ids.reshape(-1)
    group_ids = jnp.where(flat_ids < 0, 0, flat_ids).astype(jnp.int32)
    cluster_pick = flat_ids[:, None] == jnp.arange(local_count, dtype=jnp.int32)[None, :]
    live_sizes = jnp.sum(jnp.where(cluster_pick, counts[None, :], 0), axis=1)
    group_pick = group_ids[:, None] == jnp.arange(local_count, dtype=jnp.int32)[None, :]
    group_sizes = jnp.sum(group_pick.astype(jnp.int32), axis=0)
    order = jnp.argsort(group_ids, stable=True)
    undo_order = jnp.argsort(order, stable=True)
    sorted_rows = flat_rows[order]
    sorted_scores = lax.ragged_dot(
        sorted_rows, passage_blocks, group_sizes, preferred_element_type=jnp.float32
    )
    own_scores = sorted_scores[undo_order]
    centre_term = jnp.einsum(
        "rd,rd->r", flat_rows, centroids[group_ids], preferred_element_type=jnp.float32
    )
    live_mask = jnp.arange(block_span, dtype=jnp.int32)[None, :] < live_sizes[:, None]
    masked_scores = jnp.where(live_mask, own_scores + centre_term[:, None], 0.0)
    back_scores = lax.all_to_all(
        masked_scores.reshape(source_count, slot_count, block_span),
        "owner",
        split_axis=0,
        concat_axis=0,
        tiled=True,
    )
    back_sizes = lax.all_to_all(
        live_sizes.astype(jnp.float32).reshape(source_count, slot_count),
        "owner",
        split_axis=0,
        concat_axis=0,
        tiled=True,
    )
    flat_scores = back_scores.reshape(owner_count * capacity, block_span)
    scores = flat_scores[slot_index].reshape(per_device, probe_count, block_span)
    pair_sizes = back_sizes.reshape(-1)[slot_index].reshape(per_device, probe_count)
    visits = jnp.sum(pair_sizes, axis=1).astype(jnp.int32)
    return (scores, visits)


LANES = 128
GROUP = 2
TOP = 32767.0


def owner_kernel(
    n, q_ref, meta_ref, code_ref, pass_ref, cent_ref, cnt_ref,
    out_ref, vis_ref,
    pass_v, qs, ms, dense, picked, sendb, sends, recvb, recvs, words, factors, code_s, cnt_s, scale_s,
    pass_sem, qsend, msend, qrecv, mrecv, bsend, ssend, brecv, srecv, loc_sem,
):
    clusters, span, width = pass_ref.shape
    per_device, probe_count, _ = out_ref.shape
    planes = n // 4
    rows = 4 * per_device
    meta_rows, _, lane_count = meta_ref.shape
    cap = lane_count // 4
    parts = span // LANES
    half = parts // 2
    piece = per_device // 2
    me = lax.axis_index("owner")
    z = me // 4
    y = (me // 2) % 2
    c = me % 2
    y_dev = z * 4 + (1 - y) * 2 + c
    c_dev = z * 4 + y * 2 + (1 - c)
    has_low = z > 0
    has_high = z < planes - 1

    for k in range(clusters):
        pltpu.make_async_copy(pass_ref.at[k], pass_v.at[k], pass_sem.at[k]).start()

    barrier = pltpu.get_barrier_semaphore()

    def greet(dev):
        pl.semaphore_signal(barrier, inc=1, device_id={"owner": dev})

    greet(y_dev)
    greet(c_dev)

    @pl.when(has_low)
    def _():
        greet(me - 4)

    @pl.when(has_high)
    def _():
        greet(me + 4)

    pl.semaphore_wait(barrier, 2 + jnp.where(has_low, 1, 0) + jnp.where(has_high, 1, 0))

    def pair(s, h, target, dev, own=False):
        cut = pl.ds(h * piece, piece)
        query_copy = pltpu.make_async_remote_copy(
            src_ref=q_ref.at[cut] if own else qs.at[s, cut], dst_ref=qs.at[s, cut],
            send_sem=qsend.at[s, h, target], recv_sem=qrecv.at[s, h], device_id={"owner": dev},
        )
        if h == 0:
            return (query_copy,)
        return (
            query_copy,
            pltpu.make_async_remote_copy(
                src_ref=meta_ref if own else ms.at[s], dst_ref=ms.at[s],
                send_sem=msend.at[s, target], recv_sem=mrecv.at[s], device_id={"owner": dev},
            ),
        )

    def push(s, h, target, dev, own=False):
        for copy in pair(s, h, target, dev, own):
            copy.start()

    def drain(s, h, target, dev, own=False):
        for copy in pair(s, h, target, dev, own):
            copy.wait_send()

    def arrive(s, h):
        for copy in pair(s, h, 0, c_dev):
            copy.wait_recv()

    def onward(act, s, h, low, high, own=False):
        @pl.when(low)
        def _():
            act(s, h, 0, me - 4, own)

        @pl.when(high)
        def _():
            act(s, h, 1, me + 4, own)

        act(s, h, 2, y_dev, own)
        act(s, h, 3, c_dev, own)

    for h in range(2):
        onward(push, me, h, has_low, has_high, True)
    qs[me] = q_ref[...]
    ms[me] = meta_ref[...]

    near = jnp.minimum(z, planes - 1 - z)
    long_side = jnp.where(z < planes - 1 - z, 1, -1)

    def plane_of(k):
        both = jnp.where(k % 2 == 1, -1, 1) * ((k + 1) // 2)
        return z + jnp.where(k <= 2 * near, both, long_side * (k - near))

    def relay_z(k, act=push, wait=True):
        p = plane_of(k)
        s = p * 4 + y * 2 + c
        for h in range(2):
            if wait:
                arrive(s, h)
            onward(act, s, h, (p > z) & has_low, (p < z) & has_high)

    def relay_y(k):
        s = plane_of(k) * 4 + (1 - y) * 2 + c
        for h in range(2):
            arrive(s, h)
            push(s, h, 3, c_dev)

    def back_pair(s):
        return (
            pltpu.make_async_remote_copy(
                src_ref=sendb.at[pl.ds(s * cap, cap)], dst_ref=recvb.at[pl.ds(me * cap, cap)],
                send_sem=bsend.at[s], recv_sem=brecv.at[me], device_id={"owner": s},
            ),
            pltpu.make_async_remote_copy(
                src_ref=sends.at[s // 4], dst_ref=recvs.at[me],
                send_sem=ssend.at[s], recv_sem=srecv.at[me], device_id={"owner": s},
            ),
        )

    def to_scalar(s):
        return (
            pltpu.make_async_copy(ms.at[s, me // 4], code_s.at[s], loc_sem.at[0, s]),
            pltpu.make_async_copy(ms.at[s, meta_rows - 1], cnt_s.at[s], loc_sem.at[1, s]),
        )

    def compute(k):
        p = plane_of(k)
        base = p * 4
        for i in range(4):
            for copy in to_scalar(base + i):
                copy.start()
        block = qs[pl.ds(base, 4)].reshape(rows, width)
        centre = lax.dot_general(
            block, cent_ref[...], (((1,), (1,)), ((), ())), preferred_element_type=jnp.float32
        )
        lane = lax.broadcasted_iota(jnp.int32, centre.shape, 1)
        slot_lane = lax.broadcasted_iota(jnp.int32, (1, span), 1)

        def some_clusters(g, carry):
            for u in range(GROUP):
                cl = g * GROUP + u

                @pl.when(k == 0)
                def _():
                    pltpu.make_async_copy(pass_ref.at[cl], pass_v.at[cl], pass_sem.at[cl]).wait()

            for u in range(GROUP):
                cl = g * GROUP + u
                direct = lax.dot_general(
                    qs[pl.ds(base, 4)].reshape(rows, width), pass_v[cl],
                    (((1,), (1,)), ((), ())), preferred_element_type=jnp.float32,
                )
                term = jnp.sum(jnp.where(lane == cl, centre, 0.0), axis=1, keepdims=True)
                scored = jnp.where(slot_lane < cnt_ref[cl], direct + term, 0.0)
                for t in range(parts):
                    dense[pl.ds(cl * rows, rows), t, :] = scored[:, t * LANES : (t + 1) * LANES]
            return carry

        lax.fori_loop(0, clusters // GROUP, some_clusters, 0)
        for i in range(4):
            for copy in to_scalar(base + i):
                copy.wait()
        for i in range(4):
            code_lane = (me % 4) * cap

            def eight(g, carry):
                for u in range(8):
                    k_slot = g * 8 + u
                    row = code_s[base + i, 0, code_lane + k_slot] + i * per_device
                    picked[i * cap + k_slot] = dense[row]
                return carry

            lax.fori_loop(0, cap // 8, eight, 0)
        found = [picked[:, t, :] for t in range(parts)]
        peak = jnp.abs(found[0])
        for t in range(1, parts):
            peak = jnp.maximum(peak, jnp.abs(found[t]))
        top = jnp.maximum(jnp.max(peak, axis=1, keepdims=True), 1e-30)
        gain = TOP / top
        coded = [jnp.round(part * gain).astype(jnp.int32) for part in found]
        for t in range(half):
            sendb[pl.ds(base * cap, 4 * cap), t, :] = (coded[half + t] << 16) | (coded[t] & 0xFFFF)
        wide = jnp.broadcast_to(top * (1.0 / TOP), (4 * cap, LANES))
        sends[p] = jnp.transpose(wide)[0:1, :]
        for i in range(4):
            s = base + i

            @pl.when(s == me)
            def _():
                recvb[pl.ds(me * cap, cap)] = sendb[pl.ds(me * cap, cap)]
                recvs[me] = sends[p]

            @pl.when(s != me)
            def _():
                for copy in back_pair(s):
                    copy.start()

    ahead = 1 + jnp.where(near >= 1, 1, 0)

    def step(k, carry):
        @pl.when((k == 0) & (planes > 1))
        def _():
            relay_z(1)

        @pl.when((k == 0) & (ahead > 1))
        def _():
            relay_z(2)

        @pl.when((k > 0) & (k + ahead < planes))
        def _():
            relay_z(k + ahead)

        relay_y(k)
        p = plane_of(k)
        for h in range(2):
            arrive(p * 4 + y * 2 + (1 - c), h)
            arrive(p * 4 + (1 - y) * 2 + (1 - c), h)
        compute(k)
        return carry

    lax.fori_loop(0, planes, step, 0)

    def collect(s, carry):
        @pl.when(s != me)
        def _():
            for copy in (
                pltpu.make_async_remote_copy(
                    src_ref=sendb.at[pl.ds(s * cap, cap)], dst_ref=recvb.at[pl.ds(s * cap, cap)],
                    send_sem=bsend.at[s], recv_sem=brecv.at[s], device_id={"owner": c_dev},
                ),
                pltpu.make_async_remote_copy(
                    src_ref=sends.at[s // 4], dst_ref=recvs.at[s],
                    send_sem=ssend.at[s], recv_sem=srecv.at[s], device_id={"owner": c_dev},
                ),
            ):
                copy.wait_recv()

        return carry

    def count_query(q, carry):
        visited = jnp.int32(0)
        for j in range(probe_count):
            code = code_ref[q * probe_count + j]
            visited = visited + cnt_s[code >> 16, 0, (code >> 8) & 255]
        vis_ref[q] = visited
        return carry

    lax.fori_loop(0, per_device, count_query, 0)
    lax.fori_loop(0, n, collect, 0)
    scale_copy = pltpu.make_async_copy(recvs, scale_s, loc_sem.at[0, 0])
    scale_copy.start()
    scale_copy.wait()
    scale_lane = (me % 4) * cap

    def pick_query(q, carry):
        for j in range(probe_count):
            code = code_ref[q * probe_count + j]
            kept = code & 255
            words[q * probe_count + j] = recvb[(code >> 16) * cap + kept]
            factors[q * probe_count + j] = jnp.full(
                (1, LANES), scale_s[code >> 16, 0, scale_lane + kept], jnp.float32
            )
        return carry

    lax.fori_loop(0, per_device, pick_query, 0)
    factor = factors[:, 0, :]
    for t in range(half):
        word = words[:, t, :]
        low = ((word << 16) >> 16).astype(jnp.float32) * factor
        high = (word >> 16).astype(jnp.float32) * factor
        shape = (per_device, probe_count, LANES)
        out_ref[:, :, t * LANES : (t + 1) * LANES] = low.reshape(shape)
        out_ref[:, :, (half + t) * LANES : (half + t + 1) * LANES] = high.reshape(shape)

    for h in range(2):
        onward(drain, me, h, has_low, has_high, True)

    def finish(k, carry):
        @pl.when(k > 0)
        def _():
            relay_z(k, drain, False)

        for h in range(2):
            drain(plane_of(k) * 4 + (1 - y) * 2 + c, h, 3, c_dev)
        return carry

    lax.fori_loop(0, planes, finish, 0)

    def finish_back(s, carry):
        @pl.when(s != me)
        def _():
            for copy in back_pair(s):
                copy.wait_send()

        return carry

    lax.fori_loop(0, n, finish_back, 0)


def slot_tables(flat_probes, n, cap, clusters, per_device, probe_count):
    pair_count = flat_probes.shape[0]
    owner = flat_probes // clusters
    local = flat_probes % clusters
    pair = jnp.arange(pair_count, dtype=jnp.int32)
    same = (owner[:, None] == owner[None, :]) & (pair[None, :] < pair[:, None])
    slot = owner * cap + jnp.sum(same.astype(jnp.int32), axis=1)
    code = local * (4 * per_device) + pair // probe_count
    hit = slot[None, :] == jnp.arange(n * cap, dtype=jnp.int32)[:, None]
    table = jnp.sum(jnp.where(hit, code[None, :], 0), axis=1)
    return (owner << 16) | (local << 8) | (slot - owner * cap), table


def fused_body(queries, probes, passages, centroids, counts):
    n = lax.axis_size("owner")
    per_device, probe_count = probes.shape
    clusters, span, width = passages.shape
    cap = 2 * per_device * probe_count // n
    flat = probes.reshape(-1)
    codes, table = slot_tables(flat, n, cap, clusters, per_device, probe_count)
    lane_count = 4 * cap
    count_row = jnp.pad(counts, (0, lane_count - clusters)).reshape(1, 1, lane_count)
    meta = jnp.concatenate([table.reshape(n // 4, 1, lane_count), count_row], axis=0)
    vmem = pl.BlockSpec(memory_space=pltpu.VMEM)
    smem = pl.BlockSpec(memory_space=pltpu.SMEM)
    dma = pltpu.SemaphoreType.DMA
    rows = 4 * per_device
    parts = span // LANES
    return pl.pallas_call(
        lambda *refs: owner_kernel(n, *refs),
        out_shape=(
            jax.ShapeDtypeStruct((per_device, probe_count, span), jnp.float32),
            jax.ShapeDtypeStruct((per_device,), jnp.int32),
        ),
        in_specs=[vmem, vmem, smem, pl.BlockSpec(memory_space=pl.ANY), vmem, smem],
        out_specs=(vmem, smem),
        scratch_shapes=[
            pltpu.VMEM((clusters, span, width), jnp.bfloat16),
            pltpu.VMEM((n, per_device, width), jnp.bfloat16),
            pltpu.VMEM((n, n // 4 + 1, 1, lane_count), jnp.int32),
            pltpu.VMEM((clusters * rows, parts, LANES), jnp.float32),
            pltpu.VMEM((4 * cap, parts, LANES), jnp.float32),
            pltpu.VMEM((n * cap, parts // 2, LANES), jnp.int32),
            pltpu.VMEM((n // 4, 1, lane_count), jnp.float32),
            pltpu.VMEM((n * cap, parts // 2, LANES), jnp.int32),
            pltpu.VMEM((n, 1, lane_count), jnp.float32),
            pltpu.VMEM((per_device * probe_count, parts // 2, LANES), jnp.int32),
            pltpu.VMEM((per_device * probe_count, 1, LANES), jnp.float32),
            pltpu.SMEM((n, 1, lane_count), jnp.int32),
            pltpu.SMEM((n, 1, lane_count), jnp.int32),
            pltpu.SMEM((n, 1, lane_count), jnp.float32),
            dma((clusters,)),
            dma((n, 2, 4)),
            dma((n, 4)),
            dma((n, 2)),
            dma((n,)),
            dma((n,)),
            dma((n,)),
            dma((n,)),
            dma((n,)),
            dma((2, n)),
        ],
        compiler_params=pltpu.CompilerParams(
            collective_id=0, has_side_effects=True, vmem_limit_bytes=48 * 2**20
        ),
    )(queries, meta, codes, passages, centroids, counts)


def body(queries, probes, passages, centroids, counts):
    n = lax.axis_size("owner")
    per_device, probe_count = probes.shape
    clusters, span, width = passages.shape
    lane_count = 8 * per_device * probe_count // n
    held = clusters * span * (2 * width + 16 * per_device) + 2 * n * per_device * width
    fits = (
        n % 4 == 0 and n >= 8 and lane_count % LANES == 0 and lane_count >= clusters
        and span % (2 * LANES) == 0 and clusters % GROUP == 0 and clusters <= 256
        and lane_count <= 1024 and per_device % 32 == 0 and held < 32 * 2**20
    )
    chosen = fused_body if fits else routed_body
    return chosen(queries, probes, passages, centroids, counts)


def solution(mesh):
    in_specs = (
        P(("groups", "owner"), None),
        P(("groups", "owner"), None),
        P("owner", None, None),
        P("owner", None),
        P("owner"),
    )
    out_specs = (P(("groups", "owner"), None, None), P(("groups", "owner")))
    return jax.shard_map(body, mesh=mesh, in_specs=in_specs, out_specs=out_specs, check_vma=False)
```

profile of v0, /device:TPU:0, one launch (start us, length us, event | category | flops | bytes accessed | tf_op | source)
XLA Modules:
  0.0 66.3 jit_solution(7636642542997090483)
XLA Ops:
  0.6 0.7 pad.4
  1.3 0.8 %copy.8 = s32[64,8]{1,0:T(8,128)S(1)} copy(s32[64,8]{0,1:T(8,128)} %param.6) | data formatting | bytes 4096 | tf_op args[1]
  2.1 0.1 reshape.118
  2.2 0.3 convert_reduce_fusion
  2.4 0.3 select_reduce_fusion
  2.7 0.0 copy-start
  2.8 0.9 %copy-done = bf16[64,1024]{1,0:T(8,128)(2,1)S(1)} copy-done((bf16[64,1024]{1,0:T(8,128)(2,1)S(1)}, bf16[64,1024]{1,0:T(8,128)(2,1)}, u32[]{:S(2)}) %copy-start) | copy-done | bytes 131096
  3.7 0.0 copy-start.1
  3.7 0.8 %copy-done.1 = bf16[16,1024]{1,0:T(8,128)(2,1)S(1)} copy-done((bf16[16,1024]{1,0:T(8,128)(2,1)S(1)}, bf16[16,1024]{1,0:T(8,128)(2,1)}, u32[]{:S(2)}) %copy-start.1) | copy-done | bytes 32792
  4.4 0.0 copy-start.2
  4.4 0.7 copy-done.2
  5.1 59.9 %shard_map.68 = (f32[64,8,256]{2,1,0:T(8,128)S(1)}, s32[64]{0:T(128)S(1)}) custom-call(bf16[64,1024]{1,0:T(8,128)(2,1)S(1)} %copy-done, s32[5,1,256]{2,1,0:T(1,128)S(1)} %pad_add_fusion.refs_1_, s32[512]{0:T(512)S(1)} %get-tuple-element.2.refs_2_, bf16[16,256,1024]{2,1,0:T(8,128)(2,1)} %refs_3_.1, bf16[16,1024]{1,0:T(8,128)(2,1)S(1)} %copy-done.1, ...), custom_call_target="tpu_custom_call" | custom-call | tf_op jit(solution)/shard_map/pallas_call | solution.py:420
  65.0 0.8 %copy.11 = f32[64,8,256]{2,1,0:T(8,128)} copy(f32[64,8,256]{2,1,0:T(8,128)S(1)} %get-tuple-element.7) | data formatting | bytes 1048576
  65.8 0.5 copy.12
  (3 shorter events, 0.0 us)
Async XLA Ops:
  2.7 0.9 %copy-start = (bf16[64,1024]{1,0:T(8,128)(2,1)S(1)}, bf16[64,1024]{1,0:T(8,128)(2,1)}, u32[]{:S(2)}) copy-start(bf16[64,1024]{1,0:T(8,128)(2,1)} %refs_0_.1) | copy-start | bytes 393220
  3.7 0.8 %copy-start.1 = (bf16[16,1024]{1,0:T(8,128)(2,1)S(1)}, bf16[16,1024]{1,0:T(8,128)(2,1)}, u32[]{:S(2)}) copy-start(bf16[16,1024]{1,0:T(8,128)(2,1)} %refs_4_.1) | copy-start | bytes 98308
  4.4 0.7 copy-start.2
where the time goes:
time: 66.6 us; the launch traced here: 66.3 us
  Pallas kernels  59.9 us (90%)
  local copies, waits for them, and re-layouts  5.14 us (8%)
  between operations  0.67 us (1%)
    pallas_call x1, Pallas kernels, fused_body(): pl.pallas_call(lambda *refs: owner_kernel(n, *refs), out_shape=(jax.Shape...  59.9 us
    unnamed x9, local copies, waits for them, and re-layouts  4.39 us

commit v1 on v0

v1 whole, which is shorter than its diff:
```python
import jax
import jax.numpy as jnp
from jax import lax
from jax.experimental import pallas as pl
from jax.experimental.pallas import tpu as pltpu
from jax.sharding import PartitionSpec as P


def routed_body(queries, probes, passages, centroids, counts):
    owner_count = lax.axis_size("owner")
    per_device, probe_count = probes.shape
    local_count, block_span, feature_width = passages.shape
    capacity = 2 * per_device * probe_count // owner_count
    pair_count = per_device * probe_count
    passage_blocks = jnp.transpose(passages, (0, 2, 1))
    flat_probes = probes.reshape(-1)
    target_owner = flat_probes // local_count
    target_local = flat_probes % local_count
    owner_hits = (
        target_owner[:, None] == jnp.arange(owner_count, dtype=jnp.int32)[None, :]
    ).astype(jnp.int32)
    slot_rank = jnp.sum((jnp.cumsum(owner_hits, axis=0) - owner_hits) * owner_hits, axis=1)
    slot_index = target_owner * capacity + slot_rank
    pair_ids = jnp.arange(pair_count, dtype=jnp.int32)
    slot_match = slot_index[None, :] == jnp.arange(owner_count * capacity, dtype=jnp.int32)[:, None]
    slot_filled = jnp.any(slot_match, axis=1)
    source_pair = jnp.sum(jnp.where(slot_match, pair_ids[None, :], 0), axis=1)
    send_rows = jnp.where(
        slot_filled[:, None], queries[source_pair // probe_count], jnp.zeros((), jnp.bfloat16)
    )
    send_ids = jnp.where(slot_filled, target_local[source_pair], -1)
    query_rows = lax.all_to_all(
        send_rows.reshape(owner_count, capacity, feature_width),
        "owner",
        split_axis=0,
        concat_axis=0,
        tiled=True,
    )
    cluster_ids = lax.all_to_all(
        send_ids.reshape(owner_count, capacity), "owner", split_axis=0, concat_axis=0, tiled=True
    )
    source_count, slot_count = cluster_ids.shape
    row_total = source_count * slot_count
    flat_rows = query_rows.reshape(row_total, feature_width)
    flat_ids = cluster_ids.reshape(-1)
    group_ids = jnp.where(flat_ids < 0, 0, flat_ids).astype(jnp.int32)
    cluster_pick = flat_ids[:, None] == jnp.arange(local_count, dtype=jnp.int32)[None, :]
    live_sizes = jnp.sum(jnp.where(cluster_pick, counts[None, :], 0), axis=1)
    group_pick = group_ids[:, None] == jnp.arange(local_count, dtype=jnp.int32)[None, :]
    group_sizes = jnp.sum(group_pick.astype(jnp.int32), axis=0)
    order = jnp.argsort(group_ids, stable=True)
    undo_order = jnp.argsort(order, stable=True)
    sorted_rows = flat_rows[order]
    sorted_scores = lax.ragged_dot(
        sorted_rows, passage_blocks, group_sizes, preferred_element_type=jnp.float32
    )
    own_scores = sorted_scores[undo_order]
    centre_term = jnp.einsum(
        "rd,rd->r", flat_rows, centroids[group_ids], preferred_element_type=jnp.float32
    )
    live_mask = jnp.arange(block_span, dtype=jnp.int32)[None, :] < live_sizes[:, None]
    masked_scores = jnp.where(live_mask, own_scores + centre_term[:, None], 0.0)
    back_scores = lax.all_to_all(
        masked_scores.reshape(source_count, slot_count, block_span),
        "owner",
        split_axis=0,
        concat_axis=0,
        tiled=True,
    )
    back_sizes = lax.all_to_all(
        live_sizes.astype(jnp.float32).reshape(source_count, slot_count),
        "owner",
        split_axis=0,
        concat_axis=0,
        tiled=True,
    )
    flat_scores = back_scores.reshape(owner_count * capacity, block_span)
    scores = flat_scores[slot_index].reshape(per_device, probe_count, block_span)
    pair_sizes = back_sizes.reshape(-1)[slot_index].reshape(per_device, probe_count)
    visits = jnp.sum(pair_sizes, axis=1).astype(jnp.int32)
    return (scores, visits)


LANES = 128
GROUP = 4
TOP = 32767.0


def owner_kernel(
    n, q_hbm, probe_hbm, pass_hbm, cent_hbm, cnt_hbm,
    out_ref, vis_ref,
    pass_v, qs, cent_v, cnt_v, probe_v, ms, slots, rows_v, acc, cntb, sendb, sends, recvb, recvs, cnt_s,
    pass_sem, load_sem, qsend, msend, qrecv, mrecv, bsend, ssend, brecv, srecv,
):
    clusters, width = cent_v.shape
    span = pass_v.shape[0] // clusters
    probe_count, per_device = probe_v.shape
    pairs = probe_count * per_device
    planes = n // 4
    rows = 4 * per_device
    tables = ms.shape[1] - 1
    cap = LANES // 2
    wide = 4 * cap
    half = span // 2
    piece = per_device // 2
    code_bits = (clusters * per_device).bit_length() - 1
    q_bits = per_device.bit_length() - 1
    cl_bits = clusters.bit_length() - 1
    me = lax.axis_index("owner")
    z = me // 4
    y = (me // 2) % 2
    c = me % 2
    y_dev = z * 4 + (1 - y) * 2 + c
    c_dev = z * 4 + y * 2 + (1 - c)
    has_low = z > 0
    has_high = z < planes - 1

    loads = [
        pltpu.make_async_copy(q_hbm, qs.at[me], load_sem.at[0]),
        pltpu.make_async_copy(probe_hbm, probe_v, load_sem.at[1]),
        pltpu.make_async_copy(cnt_hbm, cnt_v, load_sem.at[2]),
        pltpu.make_async_copy(cent_hbm, cent_v, load_sem.at[3]),
    ]
    for copy in loads:
        copy.start()

    barrier = pltpu.get_barrier_semaphore()

    def greet(dev):
        pl.semaphore_signal(barrier, inc=1, device_id={"owner": dev})

    greet(y_dev)
    greet(c_dev)

    @pl.when(has_low)
    def _():
        greet(me - 4)

    @pl.when(has_high)
    def _():
        greet(me + 4)

    def passage_copy(k):
        return pltpu.make_async_copy(pass_hbm.at[k], pass_v.at[pl.ds(k * span, span)], pass_sem.at[k])

    for k in range(clusters):
        passage_copy(k).start()

    loads[0].wait()
    pl.semaphore_wait(barrier, 2 + jnp.where(has_low, 1, 0) + jnp.where(has_high, 1, 0))

    def chunk(s, h, target, dev):
        if h == 2:
            return pltpu.make_async_remote_copy(
                src_ref=ms.at[s], dst_ref=ms.at[s],
                send_sem=msend.at[s, target], recv_sem=mrecv.at[s], device_id={"owner": dev},
            )
        cut = pl.ds(h * piece, piece)
        return pltpu.make_async_remote_copy(
            src_ref=qs.at[s, cut], dst_ref=qs.at[s, cut],
            send_sem=qsend.at[s, h, target], recv_sem=qrecv.at[s, h], device_id={"owner": dev},
        )

    def push(s, h, target, dev):
        chunk(s, h, target, dev).start()

    def drain(s, h, target, dev):
        chunk(s, h, target, dev).wait_send()

    def arrive(s, h):
        chunk(s, h, 0, c_dev).wait_recv()

    def onward(act, s, h, low, high):
        @pl.when(low)
        def _():
            act(s, h, 0, me - 4)

        @pl.when(high)
        def _():
            act(s, h, 1, me + 4)

        act(s, h, 2, y_dev)
        act(s, h, 3, c_dev)

    for h in range(2):
        onward(push, me, h, has_low, has_high)

    for copy in loads[1:]:
        copy.wait()

    def lower(row):
        return jnp.where(c == 1, pltpu.roll(row, cap, 1), row)

    def upper(row):
        return jnp.where(c == 1, row, pltpu.roll(row, cap, 1))

    lane_row = lax.broadcasted_iota(jnp.int32, (8, LANES), 1)

    def join(first, second):
        first = jnp.broadcast_to(first, (8, LANES))
        second = jnp.broadcast_to(second, (8, LANES))
        return jnp.where(lane_row < cap, lower(first), upper(second))[0:1]

    probes = probe_v[...]
    target = probes >> cl_bits
    local = probes & (clusters - 1)
    hits = jnp.concatenate(
        [jnp.where(target == o, 1.0, 0.0).astype(jnp.float32) for o in range(n)], axis=0
    ).astype(jnp.bfloat16)
    big = n * probe_count
    r_iota = lax.broadcasted_iota(jnp.int32, (big, big), 0)
    c_iota = lax.broadcasted_iota(jnp.int32, (big, big), 1)
    p_bits = probe_count.bit_length() - 1
    earlier = jnp.where(
        ((r_iota >> p_bits) == (c_iota >> p_bits)) & (c_iota < r_iota), 1.0, 0.0
    ).astype(jnp.bfloat16)
    before = jnp.where(
        lax.broadcasted_iota(jnp.int32, (per_device, per_device), 0)
        < lax.broadcasted_iota(jnp.int32, (per_device, per_device), 1), 1.0, 0.0,
    ).astype(jnp.bfloat16)
    lead = jnp.dot(earlier, hits, preferred_element_type=jnp.float32).astype(jnp.bfloat16)
    ranks = jnp.dot(hits, before, preferred_element_type=jnp.float32) + jnp.dot(
        lead, jnp.ones((per_device, per_device), jnp.bfloat16), preferred_element_type=jnp.float32
    )
    rank = jnp.zeros((probe_count, per_device), jnp.float32)
    for o in range(n):
        rank = jnp.where(target == o, ranks[o * probe_count : (o + 1) * probe_count], rank)
    slot = target * cap + rank.astype(jnp.int32)
    code = local * per_device + lax.broadcasted_iota(jnp.int32, (probe_count, per_device), 1)
    word = (slot << code_bits) | code
    for q in range(per_device):
        slots[q * probe_count : (q + 1) * probe_count, :] = jnp.broadcast_to(
            word[:, q : q + 1], (probe_count, LANES)
        )

    def one_table(b, carry):
        lane = lax.broadcasted_iota(jnp.int32, (pairs, LANES), 1) + b * LANES
        held = slots[...]
        found = jnp.where((held >> code_bits) == lane, held & ((1 << code_bits) - 1), 0)
        ms[me, b] = jnp.sum(found.astype(jnp.float32), axis=0, keepdims=True).astype(jnp.int32)
        return carry

    lax.fori_loop(0, tables, one_table, 0)
    ms[me, tables] = jnp.zeros((1, LANES), jnp.int32)
    ms[me, tables, :, 0:clusters] = cnt_v[...]
    onward(push, me, 2, has_low, has_high)
    live_row = ms[me, tables].astype(jnp.float32)
    cntb[...] = jnp.transpose(jnp.broadcast_to(live_row, (LANES, LANES)))[0:clusters]

    near = jnp.minimum(z, planes - 1 - z)
    long_side = jnp.where(z < planes - 1 - z, 1, -1)

    def plane_of(k):
        both = jnp.where(k % 2 == 1, -1, 1) * ((k + 1) // 2)
        return z + jnp.where(k <= 2 * near, both, long_side * (k - near))

    def relay_z(k, act=push, wait=True):
        p = plane_of(k)
        s = p * 4 + y * 2 + c
        for h in range(3):
            if wait:
                arrive(s, h)
            onward(act, s, h, (p > z) & has_low, (p < z) & has_high)

    def relay_y(k):
        s = plane_of(k) * 4 + (1 - y) * 2 + c
        for h in range(3):
            arrive(s, h)
            push(s, h, 3, c_dev)

    def back_pair(s):
        return (
            pltpu.make_async_remote_copy(
                src_ref=sendb.at[pl.ds(s * cap, cap)], dst_ref=recvb.at[pl.ds(me * cap, cap)],
                send_sem=bsend.at[s], recv_sem=brecv.at[me], device_id={"owner": s},
            ),
            pltpu.make_async_remote_copy(
                src_ref=sends.at[s // 2], dst_ref=recvs.at[me],
                send_sem=ssend.at[s], recv_sem=srecv.at[me], device_id={"owner": s},
            ),
        )

    def compute(k):
        p = plane_of(k)
        base = p * 4
        codes = jnp.concatenate(
            [join(ms[base + 2 * b, me // 2], ms[base + 2 * b + 1, me // 2]) for b in range(2)], axis=1
        )
        cluster = codes >> q_bits
        block_of = lax.broadcasted_iota(jnp.int32, (1, wide), 1) // cap
        source = (codes & (per_device - 1)) + block_of * per_device
        pick = jnp.where(
            lax.broadcasted_iota(jnp.int32, (rows, wide), 0) == source, 1.0, 0.0
        ).astype(jnp.bfloat16)
        rows_v[...] = lax.dot_general(
            pick, qs[pl.ds(base, 4)].reshape(rows, width), (((0,), (0,)), ((), ())),
            preferred_element_type=jnp.float32,
        ).astype(jnp.bfloat16)
        centre = lax.dot_general(
            cent_v[...], rows_v[...], (((1,), (1,)), ((), ())), preferred_element_type=jnp.float32
        )
        mine = lax.broadcasted_iota(jnp.int32, (clusters, wide), 0) == cluster
        term = jnp.sum(jnp.where(mine, centre, 0.0), axis=0, keepdims=True)
        count_of = jnp.concatenate([cntb[...], cntb[...]], axis=1)
        live = jnp.sum(jnp.where(mine, count_of, 0.0), axis=0, keepdims=True).astype(jnp.int32)

        def some_clusters(g, carry):
            @pl.when(k == 0)
            def _():
                for u in range(GROUP):
                    passage_copy(g * GROUP + u).wait()

            tall = GROUP * span
            direct = lax.dot_general(
                pass_v[pl.ds(g * tall, tall)], rows_v[...], (((1,), (1,)), ((), ())),
                preferred_element_type=jnp.float32,
            )
            total = acc[...]
            for u in range(GROUP):
                total = jnp.where(
                    jnp.broadcast_to(cluster, (span, wide)) == g * GROUP + u,
                    direct[u * span : (u + 1) * span], total,
                )
            acc[...] = total
            return carry

        acc[...] = jnp.zeros((span, wide), jnp.float32)
        lax.fori_loop(0, clusters // GROUP, some_clusters, 0)
        place = lax.broadcasted_iota(jnp.int32, (span, wide), 0)
        value = jnp.where(place < live, acc[...] + term, 0.0)
        top = jnp.maximum(jnp.max(jnp.abs(value), axis=0, keepdims=True), 1e-30)
        coded = jnp.round(value * (TOP / top)).astype(jnp.int32)
        packed = (coded[half:] << 16) | (coded[:half] & 0xFFFF)
        sendb[pl.ds(base * cap, wide)] = jnp.transpose(packed)
        unit = top * (1.0 / TOP)
        for b in range(2):
            sends[p * 2 + b] = unit[:, b * LANES : (b + 1) * LANES]
        for i in range(4):
            s = base + i

            @pl.when(s == me)
            def _():
                recvb[pl.ds(me * cap, cap)] = sendb[pl.ds(me * cap, cap)]
                recvs[me] = sends[me // 2]

            @pl.when(s != me)
            def _():
                for copy in back_pair(s):
                    copy.start()

    ahead = 1 + jnp.where(near >= 1, 1, 0)

    def step(k, carry):
        @pl.when((k == 0) & (planes > 1))
        def _():
            relay_z(1)

        @pl.when((k == 0) & (ahead > 1))
        def _():
            relay_z(2)

        @pl.when((k > 0) & (k + ahead < planes))
        def _():
            relay_z(k + ahead)

        relay_y(k)
        p = plane_of(k)
        for h in range(3):
            arrive(p * 4 + y * 2 + (1 - c), h)
            arrive(p * 4 + (1 - y) * 2 + (1 - c), h)
        compute(k)
        return carry

    lax.fori_loop(0, planes, step, 0)

    count_copy = pltpu.make_async_copy(ms.at[:, tables], cnt_s, load_sem.at[0])
    count_copy.start()
    count_copy.wait()

    def one_owner(o, seen):
        for l in range(clusters):
            seen = jnp.where(probe_v[...] == o * clusters + l, cnt_s[o, 0, l], seen)
        return seen

    seen = lax.fori_loop(0, n, one_owner, jnp.zeros((probe_count, per_device), jnp.int32))
    vis_ref[...] = jnp.sum(seen.astype(jnp.float32), axis=0, keepdims=True).astype(jnp.int32)

    def collect(k, carry):
        p = plane_of(k)
        base = p * 4
        for i in range(4):
            s = base + i

            @pl.when(s != me)
            def _():
                for copy in (
                    pltpu.make_async_remote_copy(
                        src_ref=sendb.at[pl.ds(s * cap, cap)], dst_ref=recvb.at[pl.ds(s * cap, cap)],
                        send_sem=bsend.at[s], recv_sem=brecv.at[s], device_id={"owner": c_dev},
                    ),
                    pltpu.make_async_remote_copy(
                        src_ref=sends.at[s // 2], dst_ref=recvs.at[s],
                        send_sem=ssend.at[s], recv_sem=srecv.at[s], device_id={"owner": c_dev},
                    ),
                ):
                    copy.wait_recv()

        units = jnp.concatenate(
            [
                jnp.transpose(jnp.broadcast_to(
                    join(recvs[base + 2 * b], recvs[base + 2 * b + 1]), (LANES, LANES)
                ))
                for b in range(2)
            ],
            axis=0,
        )
        held = recvb[pl.ds(base * cap, wide)]
        value = jnp.concatenate(
            [
                ((held << 16) >> 16).astype(jnp.float32) * units,
                (held >> 16).astype(jnp.float32) * units,
            ],
            axis=1,
        )
        upper_part = value.astype(jnp.bfloat16)
        lower_part = (value - upper_part.astype(jnp.float32)).astype(jnp.bfloat16)
        at = slots[...] >> code_bits
        lane = lax.broadcasted_iota(jnp.int32, (pairs, LANES), 1) + base * cap
        chosen = jnp.concatenate(
            [jnp.where(at == lane + b * LANES, 1.0, 0.0).astype(jnp.bfloat16) for b in range(2)], axis=1
        )
        part = jnp.dot(chosen, upper_part, preferred_element_type=jnp.float32) + jnp.dot(
            chosen, lower_part, preferred_element_type=jnp.float32
        )

        @pl.when(k == 0)
        def _():
            out_ref[...] = part

        @pl.when(k > 0)
        def _():
            out_ref[...] += part

        return carry

    lax.fori_loop(0, planes, collect, 0)

    for h in range(3):
        onward(drain, me, h, has_low, has_high)

    def finish(k, carry):
        @pl.when(k > 0)
        def _():
            relay_z(k, drain, False)

        for h in range(3):
            drain(plane_of(k) * 4 + (1 - y) * 2 + c, h, 3, c_dev)
        return carry

    lax.fori_loop(0, planes, finish, 0)

    def finish_back(s, carry):
        @pl.when(s != me)
        def _():
            for copy in back_pair(s):
                copy.wait_send()

        return carry

    lax.fori_loop(0, n, finish_back, 0)


def fused_body(queries, probes, passages, centroids, counts):
    n = lax.axis_size("owner")
    per_device, probe_count = probes.shape
    clusters, span, width = passages.shape
    cap = 2 * per_device * probe_count // n
    pairs = per_device * probe_count
    tables = n * cap // LANES
    wide = 4 * cap
    vmem = pl.BlockSpec(memory_space=pltpu.VMEM)
    hbm = pl.BlockSpec(memory_space=pltpu.HBM)
    dma = pltpu.SemaphoreType.DMA
    scores, visits = pl.pallas_call(
        lambda *refs: owner_kernel(n, *refs),
        out_shape=(
            jax.ShapeDtypeStruct((pairs, span), jnp.float32),
            jax.ShapeDtypeStruct((1, per_device), jnp.int32),
        ),
        in_specs=[hbm] * 5,
        out_specs=(vmem, vmem),
        scratch_shapes=[
            pltpu.VMEM((clusters * span, width), jnp.bfloat16),
            pltpu.VMEM((n, per_device, width), jnp.bfloat16),
            pltpu.VMEM((clusters, width), jnp.bfloat16),
            pltpu.VMEM((1, clusters), jnp.int32),
            pltpu.VMEM((probe_count, per_device), jnp.int32),
            pltpu.VMEM((n, tables + 1, 1, LANES), jnp.int32),
            pltpu.VMEM((pairs, LANES), jnp.int32),
            pltpu.VMEM((wide, width), jnp.bfloat16),
            pltpu.VMEM((span, wide), jnp.float32),
            pltpu.VMEM((clusters, LANES), jnp.float32),
            pltpu.VMEM((n * cap, LANES), jnp.int32),
            pltpu.VMEM((n // 2, 1, LANES), jnp.float32),
            pltpu.VMEM((n * cap, LANES), jnp.int32),
            pltpu.VMEM((n, 1, LANES), jnp.float32),
            pltpu.SMEM((n, 1, LANES), jnp.int32),
            dma((clusters,)),
            dma((4,)),
            dma((n, 2, 4)),
            dma((n, 4)),
            dma((n, 2)),
            dma((n,)),
            dma((n,)),
            dma((n,)),
            dma((n,)),
            dma((n,)),
        ],
        compiler_params=pltpu.CompilerParams(
            collective_id=0, has_side_effects=True, vmem_limit_bytes=48 * 2**20
        ),
    )(queries, probes.T, passages, centroids, counts.reshape(1, clusters))
    return scores.reshape(per_device, probe_count, span), visits.reshape(per_device)


def power_of_two(value):
    return value > 0 and value & (value - 1) == 0


def body(queries, probes, passages, centroids, counts):
    n = lax.axis_size("owner")
    per_device, probe_count = probes.shape
    clusters, span, width = passages.shape
    cap = 2 * per_device * probe_count // n
    held = 2 * width * (clusters * span + n * per_device)
    fits = (
        n % 8 == 0 and 2 * cap == LANES and n * probe_count == LANES and span == 2 * LANES
        and power_of_two(clusters) and power_of_two(per_device) and power_of_two(probe_count)
        and clusters % GROUP == 0 and 8 <= clusters <= LANES and per_device == cap
        and clusters * per_device * n * cap < 2**23 and width % LANES == 0 and held < 32 * 2**20
    )
    chosen = fused_body if fits else routed_body
    return chosen(queries, probes, passages, centroids, counts)


def solution(mesh):
    in_specs = (
        P(("groups", "owner"), None),
        P(("groups", "owner"), None),
        P("owner", None, None),
        P("owner", None),
        P("owner"),
    )
    out_specs = (P(("groups", "owner"), None, None), P(("groups", "owner")))
    return jax.shard_map(body, mesh=mesh, in_specs=in_specs, out_specs=out_specs, check_vma=False)
```

time: 66.6 us -> 46.4 us (0.70)
  Pallas kernels: 59.9 us -> 41.2 us
  local copies, waits for them, and re-layouts: 5.14 us -> 4.3 us
    pallas_call x1, Pallas kernels: 59.9 us -> 41.2 us  [fused_body(): pl.pallas_call(lambda *refs: owner_kernel(n, *refs), out_shape=(jax.Shape...]
    unnamed x9 -> x10, local copies, waits for them, and re-layouts: 4.39 us -> 4.3 us
where the time goes in v1:
time: 46.4 us; the launch traced here: 46.1 us
  Pallas kernels  41.2 us (89%)
  local copies, waits for them, and re-layouts  4.3 us (9%)
  between operations  0.65 us (1%)
    pallas_call x1, Pallas kernels, fused_body(): pl.pallas_call(lambda *refs: owner_kernel(n, *refs), out_shape=(jax.Shape...  41.2 us
    unnamed x10, local copies, waits for them, and re-layouts  4.3 us

profile of v1, /device:TPU:0, one launch (start us, length us, event | category | flops | bytes accessed | tf_op | source)
XLA Modules:
  0.0 46.1 jit_solution(16525747296326657899)
XLA Ops:
  0.6 0.0 copy-start
  0.6 0.9 %copy-done = bf16[64,1024]{1,0:T(8,128)(2,1)S(1)} copy-done((bf16[64,1024]{1,0:T(8,128)(2,1)S(1)}, bf16[64,1024]{1,0:T(8,128)(2,1)}, u32[]{:S(2)}) %copy-start) | copy-done | bytes 131096
  1.5 0.0 copy-start.1
  1.5 0.8 %copy-done.1 = bf16[16,1024]{1,0:T(8,128)(2,1)S(1)} copy-done((bf16[16,1024]{1,0:T(8,128)(2,1)S(1)}, bf16[16,1024]{1,0:T(8,128)(2,1)}, u32[]{:S(2)}) %copy-start.1) | copy-done | bytes 32792
  2.3 0.0 copy-start.2
  2.3 0.7 %copy-done.2 = s32[64,8]{0,1:T(8,128)S(1)} copy-done((s32[64,8]{0,1:T(8,128)S(1)}, s32[64,8]{0,1:T(8,128)}, u32[]{:S(2)}) %copy-start.2) | copy-done | bytes 2072
  3.0 0.0 copy-start.3
  3.0 0.7 %copy-done.3 = s32[16]{0:T(128)S(1)} copy-done((s32[16]{0:T(128)S(1)}, s32[16]{0:T(128)}, u32[]{:S(2)}) %copy-start.3) | copy-done | bytes 88
  3.6 41.2 %shard_map.68 = (f32[512,256]{1,0:T(8,128)S(1)}, s32[1,64]{1,0:T(1,128)S(1)}) custom-call(bf16[64,1024]{1,0:T(8,128)(2,1)S(1)} %copy-done, s32[8,64]{1,0:T(8,128)S(1)} %bitcast.5, bf16[16,256,1024]{2,1,0:T(8,128)(2,1)} %refs_2_.1, bf16[16,1024]{1,0:T(8,128)(2,1)S(1)} %copy-done.1, s32[1,16]{1,0:T(1,128)S(1)} %bitcast.6), custom_call_target="tpu_custom_call" | custom-call | tf_op jit(solution)/shard_map/pallas_call | solution.py:484
  44.8 0.8 %copy.9 = f32[64,8,256]{2,1,0:T(8,128)} copy(f32[64,8,256]{2,1,0:T(8,128)S(1)} %bitcast.4) | data formatting | bytes 1048576
  45.6 0.5 %copy.10 = s32[64]{0:T(128)} copy(s32[64]{0:T(128)S(1)} %bitcast.7) | data formatting | bytes 512
Async XLA Ops:
  0.6 0.9 %copy-start = (bf16[64,1024]{1,0:T(8,128)(2,1)S(1)}, bf16[64,1024]{1,0:T(8,128)(2,1)}, u32[]{:S(2)}) copy-start(bf16[64,1024]{1,0:T(8,128)(2,1)} %refs_0_.1) | copy-start | bytes 393220
  1.5 0.8 %copy-start.1 = (bf16[16,1024]{1,0:T(8,128)(2,1)S(1)}, bf16[16,1024]{1,0:T(8,128)(2,1)}, u32[]{:S(2)}) copy-start(bf16[16,1024]{1,0:T(8,128)(2,1)} %refs_3_.1) | copy-start | bytes 98308
  2.3 0.7 %copy-start.2 = (s32[64,8]{0,1:T(8,128)S(1)}, s32[64,8]{0,1:T(8,128)}, u32[]{:S(2)}) copy-start(s32[64,8]{0,1:T(8,128)} %param.6) | copy-start | bytes 6148
  3.0 0.7 %copy-start.3 = (s32[16]{0:T(128)S(1)}, s32[16]{0:T(128)}, u32[]{:S(2)}) copy-start(s32[16]{0:T(128)} %param.9) | copy-start | bytes 196

commit v2 on v1

--- a/solution.py
+++ b/solution.py
@@ -82,18 +82,19 @@
 
 
 LANES = 128
-GROUP = 4
+GROUP = 8
 TOP = 32767.0
 
 
 def owner_kernel(
     n, q_hbm, probe_hbm, pass_hbm, cent_hbm, cnt_hbm,
     out_ref, vis_ref,
-    pass_v, qs, cent_v, cnt_v, probe_v, ms, slots, rows_v, acc, cntb, sendb, sends, recvb, recvs, cnt_s,
+    pass_v, qs, centre_v, cnt_v, probe_v, ms, slots, rows_v, acc, cntb, sendb, sends, recvb, recvs, cnt_s,
     pass_sem, load_sem, qsend, msend, qrecv, mrecv, bsend, ssend, brecv, srecv,
 ):
-    clusters, width = cent_v.shape
-    span = pass_v.shape[0] // clusters
+    clusters, width = cent_hbm.shape
+    span = pass_hbm.shape[1]
+    tall = GROUP * span
     probe_count, per_device = probe_v.shape
     pairs = probe_count * per_device
     planes = n // 4
@@ -119,7 +120,9 @@
         pltpu.make_async_copy(q_hbm, qs.at[me], load_sem.at[0]),
         pltpu.make_async_copy(probe_hbm, probe_v, load_sem.at[1]),
         pltpu.make_async_copy(cnt_hbm, cnt_v, load_sem.at[2]),
-        pltpu.make_async_copy(cent_hbm, cent_v, load_sem.at[3]),
+    ] + [
+        pltpu.make_async_copy(cent_hbm, pass_v.at[g, pl.ds(tall, clusters)], load_sem.at[3 + g])
+        for g in range(clusters // GROUP)
     ]
     for copy in loads:
         copy.start()
@@ -141,7 +144,7 @@
         greet(me + 4)
 
     def passage_copy(k):
-        return pltpu.make_async_copy(pass_hbm.at[k], pass_v.at[pl.ds(k * span, span)], pass_sem.at[k])
+        return pltpu.make_async_copy(pass_hbm.at[k], pass_v.at[k // GROUP, pl.ds((k % GROUP) * span, span)], pass_sem.at[k])
 
     for k in range(clusters):
         passage_copy(k).start()
@@ -182,8 +185,7 @@
         act(s, h, 2, y_dev)
         act(s, h, 3, c_dev)
 
-    for h in range(2):
-        onward(push, me, h, has_low, has_high)
+    onward(push, me, 0, has_low, has_high)
 
     for copy in loads[1:]:
         copy.wait()
@@ -244,29 +246,82 @@
     ms[me, tables] = jnp.zeros((1, LANES), jnp.int32)
     ms[me, tables, :, 0:clusters] = cnt_v[...]
     onward(push, me, 2, has_low, has_high)
+    onward(push, me, 1, has_low, has_high)
     live_row = ms[me, tables].astype(jnp.float32)
     cntb[...] = jnp.transpose(jnp.broadcast_to(live_row, (LANES, LANES)))[0:clusters]
 
     near = jnp.minimum(z, planes - 1 - z)
     long_side = jnp.where(z < planes - 1 - z, 1, -1)
 
+    far = planes - 1 - near
+
     def plane_of(k):
-        both = jnp.where(k % 2 == 1, -1, 1) * ((k + 1) // 2)
-        return z + jnp.where(k <= 2 * near, both, long_side * (k - near))
-
-    def relay_z(k, act=push, wait=True):
+        return z + long_side * jnp.where(k <= far, k, far - k)
+
+    def collect_of(k):
+        ends = jnp.where(k == 1, 2, jnp.where(k == 2, 1, k))
+        inner = jnp.where(k == 1, -1, jnp.where(k > 1, k - 1, 0))
+        return z + long_side * jnp.where(near == 0, ends, inner)
+
+    def pick_of(u, values):
+        found = values[0]
+        for at in range(1, len(values)):
+            found = jnp.where(u == at, values[at], found)
+        return found
+
+    def chips_of(u):
+        inner = near > 0
+        first = pick_of(u, (0, 2, jnp.where(inner, 0, 3), jnp.where(inner, 3, 2)))
+        first_far = pick_of(u, (0, 0, jnp.where(inner, 1, 0), jnp.where(inner, 0, 1)))
+        second = pick_of(u, (1, jnp.where(inner, 1, 0), jnp.where(inner, 2, 1), 3))
+        second_far = jnp.where(u == 0, 0, 1)
+
+        def chip(k, other):
+            return plane_of(k) * 2 + jnp.where(other == 1, 1 - y, y)
+
+        return chip(first, first_far), chip(second, second_far)
+
+    def along(k):
+        return plane_of(k) * 4 + y * 2 + c
+
+    def forward_z(k, h, act=push, wait=True):
         p = plane_of(k)
-        s = p * 4 + y * 2 + c
-        for h in range(3):
-            if wait:
-                arrive(s, h)
-            onward(act, s, h, (p > z) & has_low, (p < z) & has_high)
-
-    def relay_y(k):
+        if wait:
+            arrive(along(k), h)
+
+        @pl.when((p > z) & has_low)
+        def _():
+            act(along(k), h, 0, me - 4)
+
+        @pl.when((p < z) & has_high)
+        def _():
+            act(along(k), h, 1, me + 4)
+
+    def forward_y(k, h, act=push):
+        act(along(k), h, 2, y_dev)
+
+    def forward_c(k, h, act=push):
+        act(along(k), h, 3, c_dev)
+
+    def forward_plane(k, h, act=push):
+        forward_y(k, h, act)
+        forward_c(k, h, act)
+
+    def relay_y(k, h):
         s = plane_of(k) * 4 + (1 - y) * 2 + c
-        for h in range(3):
-            arrive(s, h)
-            push(s, h, 3, c_dev)
+        arrive(s, h)
+        push(s, h, 3, c_dev)
+
+    def service(u, pieces):
+        for h in pieces:
+            @pl.when(u + 2 <= far)
+            def _():
+                forward_z(u + 2, h)
+                forward_plane(u + 2, h)
+
+            @pl.when(u + 1 < planes)
+            def _():
+                relay_y(u + 1, h)
 
     def back_pair(s):
         return (
@@ -281,10 +336,9 @@
         )
 
     def compute(k):
-        p = plane_of(k)
-        base = p * 4
+        chips = chips_of(k)
         codes = jnp.concatenate(
-            [join(ms[base + 2 * b, me // 2], ms[base + 2 * b + 1, me // 2]) for b in range(2)], axis=1
+            [join(ms[2 * chip, me // 2], ms[2 * chip + 1, me // 2]) for chip in chips], axis=1
         )
         cluster = codes >> q_bits
         block_of = lax.broadcasted_iota(jnp.int32, (1, wide), 1) // cap
@@ -292,27 +346,21 @@
         pick = jnp.where(
             lax.broadcasted_iota(jnp.int32, (rows, wide), 0) == source, 1.0, 0.0
         ).astype(jnp.bfloat16)
+        block = jnp.concatenate(
+            [qs[pl.ds(2 * chip, 2)].reshape(2 * per_device, width) for chip in chips], axis=0
+        )
         rows_v[...] = lax.dot_general(
-            pick, qs[pl.ds(base, 4)].reshape(rows, width), (((0,), (0,)), ((), ())),
+            pick, block, (((0,), (0,)), ((), ())),
             preferred_element_type=jnp.float32,
         ).astype(jnp.bfloat16)
-        centre = lax.dot_general(
-            cent_v[...], rows_v[...], (((1,), (1,)), ((), ())), preferred_element_type=jnp.float32
-        )
-        mine = lax.broadcasted_iota(jnp.int32, (clusters, wide), 0) == cluster
-        term = jnp.sum(jnp.where(mine, centre, 0.0), axis=0, keepdims=True)
-        count_of = jnp.concatenate([cntb[...], cntb[...]], axis=1)
-        live = jnp.sum(jnp.where(mine, count_of, 0.0), axis=0, keepdims=True).astype(jnp.int32)
-
         def some_clusters(g, carry):
             @pl.when(k == 0)
             def _():
                 for u in range(GROUP):
                     passage_copy(g * GROUP + u).wait()
 
-            tall = GROUP * span
             direct = lax.dot_general(
-                pass_v[pl.ds(g * tall, tall)], rows_v[...], (((1,), (1,)), ((), ())),
+                pass_v[g], rows_v[...], (((1,), (1,)), ((), ())),
                 preferred_element_type=jnp.float32,
             )
             total = acc[...]
@@ -322,21 +370,47 @@
                     direct[u * span : (u + 1) * span], total,
                 )
             acc[...] = total
+            centre_v[...] = direct[tall:]
+
+            @pl.when(g == 0)
+            def _():
+                service(k, (0, 2))
+
+                @pl.when(k > 0)
+                def _():
+                    service(k, (1,))
+
+            @pl.when(g == 1)
+            def _():
+                @pl.when(k == 0)
+                def _():
+                    service(k, (1,))
+
+                @pl.when((k == 0) & (near > 0))
+                def _():
+                    for h in (0, 2, 1):
+                        forward_y(planes - 1, h)
+
             return carry
 
         acc[...] = jnp.zeros((span, wide), jnp.float32)
         lax.fori_loop(0, clusters // GROUP, some_clusters, 0)
+        mine = lax.broadcasted_iota(jnp.int32, (clusters, wide), 0) == cluster
+        term = jnp.sum(jnp.where(mine, centre_v[...], 0.0), axis=0, keepdims=True)
+        count_of = jnp.concatenate([cntb[...], cntb[...]], axis=1)
+        live = jnp.sum(jnp.where(mine, count_of, 0.0), axis=0, keepdims=True).astype(jnp.int32)
         place = lax.broadcasted_iota(jnp.int32, (span, wide), 0)
         value = jnp.where(place < live, acc[...] + term, 0.0)
         top = jnp.maximum(jnp.max(jnp.abs(value), axis=0, keepdims=True), 1e-30)
         coded = jnp.round(value * (TOP / top)).astype(jnp.int32)
         packed = (coded[half:] << 16) | (coded[:half] & 0xFFFF)
-        sendb[pl.ds(base * cap, wide)] = jnp.transpose(packed)
+        turned = jnp.transpose(packed)
         unit = top * (1.0 / TOP)
-        for b in range(2):
-            sends[p * 2 + b] = unit[:, b * LANES : (b + 1) * LANES]
+        for b, chip in enumerate(chips):
+            sendb[pl.ds(2 * chip * cap, LANES)] = turned[b * LANES : (b + 1) * LANES]
+            sends[chip] = unit[:, b * LANES : (b + 1) * LANES]
         for i in range(4):
-            s = base + i
+            s = 2 * chips[i // 2] + i % 2
 
             @pl.when(s == me)
             def _():
@@ -348,33 +422,33 @@
                 for copy in back_pair(s):
                     copy.start()
 
-    ahead = 1 + jnp.where(near >= 1, 1, 0)
+    for h in (0, 2, 1):
+        forward_z(1, h)
+        forward_plane(1, h)
+
+        @pl.when(near > 0)
+        def _():
+            forward_z(planes - 1, h)
+            forward_c(planes - 1, h)
+
+        relay_y(0, h)
+
+    count_copy = pltpu.make_async_copy(ms.at[:, tables], cnt_s, load_sem.at[0])
 
     def step(k, carry):
-        @pl.when((k == 0) & (planes > 1))
-        def _():
-            relay_z(1)
-
-        @pl.when((k == 0) & (ahead > 1))
-        def _():
-            relay_z(2)
-
-        @pl.when((k > 0) & (k + ahead < planes))
-        def _():
-            relay_z(k + ahead)
-
-        relay_y(k)
-        p = plane_of(k)
-        for h in range(3):
-            arrive(p * 4 + y * 2 + (1 - c), h)
-            arrive(p * 4 + (1 - y) * 2 + (1 - c), h)
+        for chip in chips_of(k):
+            for h in range(3):
+                arrive(2 * chip + (1 - c), h)
+
+        @pl.when(k == planes - 1)
+        def _():
+            count_copy.start()
+
         compute(k)
         return carry
 
     lax.fori_loop(0, planes, step, 0)
 
-    count_copy = pltpu.make_async_copy(ms.at[:, tables], cnt_s, load_sem.at[0])
-    count_copy.start()
     count_copy.wait()
 
     def one_owner(o, seen):
@@ -386,7 +460,7 @@
     vis_ref[...] = jnp.sum(seen.astype(jnp.float32), axis=0, keepdims=True).astype(jnp.int32)
 
     def collect(k, carry):
-        p = plane_of(k)
+        p = collect_of(k)
         base = p * 4
         for i in range(4):
             s = base + i
@@ -451,7 +525,9 @@
     def finish(k, carry):
         @pl.when(k > 0)
         def _():
-            relay_z(k, drain, False)
+            for h in range(3):
+                forward_z(k, h, drain, False)
+                forward_plane(k, h, drain)
 
         for h in range(3):
             drain(plane_of(k) * 4 + (1 - y) * 2 + c, h, 3, c_dev)
@@ -490,9 +566,9 @@
         in_specs=[hbm] * 5,
         out_specs=(vmem, vmem),
         scratch_shapes=[
-            pltpu.VMEM((clusters * span, width), jnp.bfloat16),
+            pltpu.VMEM((clusters // GROUP, GROUP * span + clusters, width), jnp.bfloat16),
             pltpu.VMEM((n, per_device, width), jnp.bfloat16),
-            pltpu.VMEM((clusters, width), jnp.bfloat16),
+            pltpu.VMEM((clusters, wide), jnp.float32),
             pltpu.VMEM((1, clusters), jnp.int32),
             pltpu.VMEM((probe_count, per_device), jnp.int32),
             pltpu.VMEM((n, tables + 1, 1, LANES), jnp.int32),
@@ -506,7 +582,7 @@
             pltpu.VMEM((n, 1, LANES), jnp.float32),
             pltpu.SMEM((n, 1, LANES), jnp.int32),
             dma((clusters,)),
-            dma((4,)),
+            dma((3 + clusters // GROUP,)),
             dma((n, 2, 4)),
             dma((n, 4)),
             dma((n, 2)),
@@ -519,7 +595,7 @@
         compiler_params=pltpu.CompilerParams(
             collective_id=0, has_side_effects=True, vmem_limit_bytes=48 * 2**20
         ),
-    )(queries, probes.T, passages, centroids, counts.reshape(1, clusters))
+    )(*[pltpu.with_memory_space_constraint(v, pltpu.HBM) for v in (queries, probes.T, passages, centroids, counts.reshape(1, clusters))])
     return scores.reshape(per_device, probe_count, span), visits.reshape(per_device)
 
 
@@ -534,9 +610,9 @@
     cap = 2 * per_device * probe_count // n
     held = 2 * width * (clusters * span + n * per_device)
     fits = (
-        n % 8 == 0 and 2 * cap == LANES and n * probe_count == LANES and span == 2 * LANES
+        n == 16 and clusters % 16 == 0 and 2 * cap == LANES and n * probe_count == LANES and span == 2 * LANES
         and power_of_two(clusters) and power_of_two(per_device) and power_of_two(probe_count)
-        and clusters % GROUP == 0 and 8 <= clusters <= LANES and per_device == cap
+        and clusters % GROUP == 0 and clusters <= LANES and per_device == cap
         and clusters * per_device * n * cap < 2**23 and width % LANES == 0 and held < 32 * 2**20
     )
     chosen = fused_body if fits else routed_body

time: 46.4 us -> 38.2 us (0.82)
  Pallas kernels: 41.2 us -> 36.1 us
  local copies, waits for them, and re-layouts: 4.3 us -> 1.31 us
    pallas_call x1, Pallas kernels: 41.2 us -> 36.1 us  [fused_body(): pl.pallas_call(lambda *refs: owner_kernel(n, *refs), out_shape=(jax.Shape...]
    unnamed x10 -> x2, local copies, waits for them, and re-layouts: 4.3 us -> 1.31 us
where the time goes in v2:
time: 38.2 us; the launch traced here: 38 us
  Pallas kernels  36.1 us (95%)
  local copies, waits for them, and re-layouts  1.31 us (3%)
  between operations  0.64 us (2%)
    pallas_call x1, Pallas kernels, fused_body(): pl.pallas_call(lambda *refs: owner_kernel(n, *refs), out_shape=(jax.Shape...  36.1 us
    unnamed x2, local copies, waits for them, and re-layouts  1.31 us

profile of v2, /device:TPU:0, one launch (start us, length us, event | category | flops | bytes accessed | tf_op | source)
XLA Modules:
  0.0 38.0 jit_solution(57666962218809821)
XLA Ops:
  0.6 36.1 %shard_map.68 = (f32[512,256]{1,0:T(8,128)S(1)}, s32[1,64]{1,0:T(1,128)S(1)}) custom-call(bf16[64,1024]{1,0:T(8,128)(2,1)} %refs_0_.1, s32[8,64]{1,0:T(8,128)} %bitcast.6, bf16[16,256,1024]{2,1,0:T(8,128)(2,1)} %refs_2_.1, bf16[16,1024]{1,0:T(8,128)(2,1)} %refs_3_.1, s32[1,16]{1,0:T(1,128)} %bitcast.7), custom_call_target="tpu_custom_call" | custom-call | tf_op jit(solution)/shard_map/pallas_call | solution.py:560
  36.7 0.8 %copy.9 = f32[64,8,256]{2,1,0:T(8,128)} copy(f32[64,8,256]{2,1,0:T(8,128)S(1)} %bitcast.4) | data formatting | bytes 1048576
  37.5 0.5 %copy.10 = s32[64]{0:T(128)} copy(s32[64]{0:T(128)S(1)} %bitcast.5) | data formatting | bytes 512

commit v3 on v2

--- a/solution.py
+++ b/solution.py
@@ -82,19 +82,17 @@
 
 
 LANES = 128
-GROUP = 8
 TOP = 32767.0
 
 
 def owner_kernel(
     n, q_hbm, probe_hbm, pass_hbm, cent_hbm, cnt_hbm,
     out_ref, vis_ref,
-    pass_v, qs, centre_v, cnt_v, probe_v, ms, slots, rows_v, acc, cntb, sendb, sends, recvb, recvs, cnt_s,
+    pass_v, qs, cnt_v, probe_v, ms, slots, rows_v, acc, cntb, sendb, sends, recvb, recvs, cnt_s,
     pass_sem, load_sem, qsend, msend, qrecv, mrecv, bsend, ssend, brecv, srecv,
 ):
     clusters, width = cent_hbm.shape
     span = pass_hbm.shape[1]
-    tall = GROUP * span
     probe_count, per_device = probe_v.shape
     pairs = probe_count * per_device
     planes = n // 4
@@ -103,6 +101,7 @@
     cap = LANES // 2
     wide = 4 * cap
     half = span // 2
+    short = cap // 2
     piece = per_device // 2
     code_bits = (clusters * per_device).bit_length() - 1
     q_bits = per_device.bit_length() - 1
@@ -120,9 +119,6 @@
         pltpu.make_async_copy(q_hbm, qs.at[me], load_sem.at[0]),
         pltpu.make_async_copy(probe_hbm, probe_v, load_sem.at[1]),
         pltpu.make_async_copy(cnt_hbm, cnt_v, load_sem.at[2]),
-    ] + [
-        pltpu.make_async_copy(cent_hbm, pass_v.at[g, pl.ds(tall, clusters)], load_sem.at[3 + g])
-        for g in range(clusters // GROUP)
     ]
     for copy in loads:
         copy.start()
@@ -143,11 +139,19 @@
     def _():
         greet(me + 4)
 
-    def passage_copy(k):
-        return pltpu.make_async_copy(pass_hbm.at[k], pass_v.at[k // GROUP, pl.ds((k % GROUP) * span, span)], pass_sem.at[k])
-
-    for k in range(clusters):
-        passage_copy(k).start()
+    def passage_copies(g):
+        return [
+            pltpu.make_async_copy(
+                pass_hbm.at[k, pl.ds(g * half, half)], pass_v.at[g, pl.ds(k * half, half)], pass_sem.at[g]
+            )
+            for k in range(clusters)
+        ] + [
+            pltpu.make_async_copy(cent_hbm, pass_v.at[g, pl.ds(clusters * half, clusters)], pass_sem.at[g])
+        ]
+
+    for g in range(2):
+        for copy in passage_copies(g):
+            copy.start()
 
     loads[0].wait()
     pl.semaphore_wait(barrier, 2 + jnp.where(has_low, 1, 0) + jnp.where(has_high, 1, 0))
@@ -156,19 +160,23 @@
         if h == 2:
             return pltpu.make_async_remote_copy(
                 src_ref=ms.at[s], dst_ref=ms.at[s],
-                send_sem=msend.at[s, target], recv_sem=mrecv.at[s], device_id={"owner": dev},
+                send_sem=msend.at[max(target - 1, 0)], recv_sem=mrecv.at[s], device_id={"owner": dev},
             )
         cut = pl.ds(h * piece, piece)
         return pltpu.make_async_remote_copy(
             src_ref=qs.at[s, cut], dst_ref=qs.at[s, cut],
-            send_sem=qsend.at[s, h, target], recv_sem=qrecv.at[s, h], device_id={"owner": dev},
+            send_sem=qsend.at[max(target - 1, 0)], recv_sem=qrecv.at[s, h], device_id={"owner": dev},
         )
 
     def push(s, h, target, dev):
         chunk(s, h, target, dev).start()
 
-    def drain(s, h, target, dev):
-        chunk(s, h, target, dev).wait_send()
+    def drain(way, blocks):
+        for ref, sem in ((qs, qsend), (ms, msend)):
+            pltpu.make_async_remote_copy(
+                src_ref=ref.at[pl.ds(0, blocks)], dst_ref=ref.at[pl.ds(0, blocks)],
+                send_sem=sem.at[way], recv_sem=mrecv.at[0], device_id={"owner": c_dev},
+            ).wait_send()
 
     def arrive(s, h):
         chunk(s, h, 0, c_dev).wait_recv()
@@ -323,17 +331,26 @@
             def _():
                 relay_y(u + 1, h)
 
-    def back_pair(s):
+    def back_pair(g, s):
         return (
             pltpu.make_async_remote_copy(
-                src_ref=sendb.at[pl.ds(s * cap, cap)], dst_ref=recvb.at[pl.ds(me * cap, cap)],
-                send_sem=bsend.at[s], recv_sem=brecv.at[me], device_id={"owner": s},
+                src_ref=sendb.at[g, pl.ds(s * short, short)],
+                dst_ref=recvb.at[g, pl.ds(me * short, short)],
+                send_sem=bsend.at[g], recv_sem=brecv.at[z], device_id={"owner": s},
             ),
             pltpu.make_async_remote_copy(
-                src_ref=sends.at[s // 2], dst_ref=recvs.at[me],
-                send_sem=ssend.at[s], recv_sem=srecv.at[me], device_id={"owner": s},
+                src_ref=sends.at[g, s], dst_ref=recvs.at[g, me],
+                send_sem=ssend.at[g], recv_sem=srecv.at[z], device_id={"owner": s},
             ),
         )
+
+    def back_arrive(p, first, owners):
+        for ref, sem, each in ((recvb, brecv, short), (recvs, srecv, 1)):
+            cut = pl.ds(first * each, owners * each)
+            pltpu.make_async_remote_copy(
+                src_ref=ref.at[:, cut], dst_ref=ref.at[:, cut],
+                send_sem=bsend.at[0], recv_sem=sem.at[p], device_id={"owner": c_dev},
+            ).wait_recv()
 
     def compute(k):
         chips = chips_of(k)
@@ -350,77 +367,70 @@
             [qs[pl.ds(2 * chip, 2)].reshape(2 * per_device, width) for chip in chips], axis=0
         )
         rows_v[...] = lax.dot_general(
-            pick, block, (((0,), (0,)), ((), ())),
-            preferred_element_type=jnp.float32,
+            block, pick, (((0,), (0,)), ((), ())), preferred_element_type=jnp.float32
         ).astype(jnp.bfloat16)
-        def some_clusters(g, carry):
+        count_of = jnp.concatenate([cntb[...], cntb[...]], axis=1)
+
+        def one_half(g, carry):
             @pl.when(k == 0)
             def _():
-                for u in range(GROUP):
-                    passage_copy(g * GROUP + u).wait()
+                pltpu.make_async_copy(pass_v.at[g], pass_v.at[g], pass_sem.at[g]).wait()
 
             direct = lax.dot_general(
-                pass_v[g], rows_v[...], (((1,), (1,)), ((), ())),
-                preferred_element_type=jnp.float32,
+                pass_v[g], rows_v[...], (((1,), (0,)), ((), ())), preferred_element_type=jnp.float32
             )
-            total = acc[...]
-            for u in range(GROUP):
+            total = direct[:half]
+            for u in range(1, clusters):
                 total = jnp.where(
-                    jnp.broadcast_to(cluster, (span, wide)) == g * GROUP + u,
-                    direct[u * span : (u + 1) * span], total,
+                    jnp.broadcast_to(cluster, (half, wide)) == u, direct[u * half : (u + 1) * half], total
                 )
             acc[...] = total
-            centre_v[...] = direct[tall:]
+            mine = lax.broadcasted_iota(jnp.int32, (clusters, wide), 0) == cluster
+            term = jnp.sum(jnp.where(mine, direct[clusters * half :], 0.0), axis=0, keepdims=True)
+            live = jnp.sum(jnp.where(mine, count_of, 0.0), axis=0, keepdims=True).astype(jnp.int32)
+            place = lax.broadcasted_iota(jnp.int32, (half, wide), 0) + g * half
+            value = jnp.where(place < live, acc[...] + term, 0.0)
+            top = jnp.maximum(jnp.max(jnp.abs(value), axis=0, keepdims=True), 1e-30)
+            coded = jnp.round(value * (TOP / top)).astype(jnp.int32)
+            unit = top * (1.0 / TOP)
+            for b, chip in enumerate(chips):
+                part = coded[:, b * LANES : (b + 1) * LANES]
+                packed = (pltpu.roll(part, LANES - short, 1) << 16) | (part & 0xFFFF)
+                turned = jnp.transpose(packed)
+                lane_unit = jnp.broadcast_to(unit[:, b * LANES : (b + 1) * LANES], (8, LANES))
+                other = pltpu.roll(lane_unit, cap, 1)
+                for i in range(2):
+                    sendb[g, pl.ds((2 * chip + i) * short, short)] = turned[i * cap : i * cap + short]
+                    sends[g, 2 * chip + i] = jnp.where((lane_row < cap) == (i == 0), lane_unit, other)[0:1]
+            for i in range(4):
+                s = 2 * chips[i // 2] + i % 2
+
+                @pl.when(s == me)
+                def _():
+                    recvb[g, pl.ds(me * short, short)] = sendb[g, pl.ds(me * short, short)]
+                    recvs[g, me] = sends[g, me]
+
+                @pl.when(s != me)
+                def _():
+                    for copy in back_pair(g, s):
+                        copy.start()
 
             @pl.when(g == 0)
             def _():
                 service(k, (0, 2))
 
-                @pl.when(k > 0)
-                def _():
-                    service(k, (1,))
-
-            @pl.when(g == 1)
+            @pl.when((g == 0) == (k > 0))
             def _():
-                @pl.when(k == 0)
-                def _():
-                    service(k, (1,))
-
-                @pl.when((k == 0) & (near > 0))
-                def _():
-                    for h in (0, 2, 1):
-                        forward_y(planes - 1, h)
+                service(k, (1,))
+
+            @pl.when((g == 1) & (k == 0) & (near > 0))
+            def _():
+                for h in (0, 2, 1):
+                    forward_y(planes - 1, h)
 
             return carry
 
-        acc[...] = jnp.zeros((span, wide), jnp.float32)
-        lax.fori_loop(0, clusters // GROUP, some_clusters, 0)
-        mine = lax.broadcasted_iota(jnp.int32, (clusters, wide), 0) == cluster
-        term = jnp.sum(jnp.where(mine, centre_v[...], 0.0), axis=0, keepdims=True)
-        count_of = jnp.concatenate([cntb[...], cntb[...]], axis=1)
-        live = jnp.sum(jnp.where(mine, count_of, 0.0), axis=0, keepdims=True).astype(jnp.int32)
-        place = lax.broadcasted_iota(jnp.int32, (span, wide), 0)
-        value = jnp.where(place < live, acc[...] + term, 0.0)
-        top = jnp.maximum(jnp.max(jnp.abs(value), axis=0, keepdims=True), 1e-30)
-        coded = jnp.round(value * (TOP / top)).astype(jnp.int32)
-        packed = (coded[half:] << 16) | (coded[:half] & 0xFFFF)
-        turned = jnp.transpose(packed)
-        unit = top * (1.0 / TOP)
-        for b, chip in enumerate(chips):
-            sendb[pl.ds(2 * chip * cap, LANES)] = turned[b * LANES : (b + 1) * LANES]
-            sends[chip] = unit[:, b * LANES : (b + 1) * LANES]
-        for i in range(4):
-            s = 2 * chips[i // 2] + i % 2
-
-            @pl.when(s == me)
-            def _():
-                recvb[pl.ds(me * cap, cap)] = sendb[pl.ds(me * cap, cap)]
-                recvs[me] = sends[me // 2]
-
-            @pl.when(s != me)
-            def _():
-                for copy in back_pair(s):
-                    copy.start()
+        lax.fori_loop(0, 2, one_half, 0)
 
     for h in (0, 2, 1):
         forward_z(1, h)
@@ -462,46 +472,37 @@
     def collect(k, carry):
         p = collect_of(k)
         base = p * 4
-        for i in range(4):
-            s = base + i
-
-            @pl.when(s != me)
-            def _():
-                for copy in (
-                    pltpu.make_async_remote_copy(
-                        src_ref=sendb.at[pl.ds(s * cap, cap)], dst_ref=recvb.at[pl.ds(s * cap, cap)],
-                        send_sem=bsend.at[s], recv_sem=brecv.at[s], device_id={"owner": c_dev},
-                    ),
-                    pltpu.make_async_remote_copy(
-                        src_ref=sends.at[s // 2], dst_ref=recvs.at[s],
-                        send_sem=ssend.at[s], recv_sem=srecv.at[s], device_id={"owner": c_dev},
-                    ),
-                ):
-                    copy.wait_recv()
-
-        units = jnp.concatenate(
-            [
-                jnp.transpose(jnp.broadcast_to(
-                    join(recvs[base + 2 * b], recvs[base + 2 * b + 1]), (LANES, LANES)
-                ))
-                for b in range(2)
-            ],
-            axis=0,
-        )
-        held = recvb[pl.ds(base * cap, wide)]
-        value = jnp.concatenate(
-            [
-                ((held << 16) >> 16).astype(jnp.float32) * units,
-                (held >> 16).astype(jnp.float32) * units,
-            ],
-            axis=1,
-        )
+        @pl.when(p == z)
+        def _():
+            back_arrive(p, base, 3)
+
+        @pl.when(p != z)
+        def _():
+            back_arrive(p, base, 4)
+
+        quarter = lax.broadcasted_iota(jnp.int32, (8, LANES), 1) // short
+        columns = []
+        for g in range(2):
+            straight = [jnp.broadcast_to(recvs[g, base + i], (8, LANES)) for i in range(4)]
+            shifted = [pltpu.roll(row, short, 1) for row in straight]
+            held = recvb[g, pl.ds(base * short, LANES)]
+            halves = []
+            for high in range(2):
+                unit = jnp.zeros((8, LANES), jnp.float32)
+                for i in range(4):
+                    unit = jnp.where(quarter == i, straight[i] if i % 2 == high else shifted[i], unit)
+                units = jnp.transpose(jnp.broadcast_to(unit[0:1], (LANES, LANES)))
+                number = held >> 16 if high else (held << 16) >> 16
+                halves.append(number.astype(jnp.float32) * units)
+            columns.append(jnp.concatenate(halves, axis=0))
+        value = jnp.concatenate(columns, axis=1)
         upper_part = value.astype(jnp.bfloat16)
         lower_part = (value - upper_part.astype(jnp.float32)).astype(jnp.bfloat16)
         at = slots[...] >> code_bits
-        lane = lax.broadcasted_iota(jnp.int32, (pairs, LANES), 1) + base * cap
+        lane = lax.broadcasted_iota(jnp.int32, (pairs, LANES), 1)
+        lane = (lane // short + base) * cap + lane % short
         chosen = jnp.concatenate(
-            [jnp.where(at == lane + b * LANES, 1.0, 0.0).astype(jnp.bfloat16) for b in range(2)], axis=1
+            [jnp.where(at == lane + b * short, 1.0, 0.0).astype(jnp.bfloat16) for b in range(2)], axis=1
         )
         part = jnp.dot(chosen, upper_part, preferred_element_type=jnp.float32) + jnp.dot(
             chosen, lower_part, preferred_element_type=jnp.float32
@@ -519,31 +520,23 @@
 
     lax.fori_loop(0, planes, collect, 0)
 
-    for h in range(3):
-        onward(drain, me, h, has_low, has_high)
-
-    def finish(k, carry):
-        @pl.when(k > 0)
-        def _():
-            for h in range(3):
-                forward_z(k, h, drain, False)
-                forward_plane(k, h, drain)
-
-        for h in range(3):
-            drain(plane_of(k) * 4 + (1 - y) * 2 + c, h, 3, c_dev)
-        return carry
-
-    lax.fori_loop(0, planes, finish, 0)
-
-    def finish_back(s, carry):
-        @pl.when(s != me)
-        def _():
-            for copy in back_pair(s):
-                copy.wait_send()
-
-        return carry
-
-    lax.fori_loop(0, n, finish_back, 0)
+    @pl.when(near > 0)
+    def _():
+        drain(0, planes + 1)
+
+    @pl.when(near == 0)
+    def _():
+        drain(0, 1)
+
+    drain(1, planes)
+    drain(2, 2 * planes)
+    for g in range(2):
+        for ref, sem, each in ((sendb, bsend, short), (sends, ssend, 1)):
+            cut = ref.at[g, pl.ds(0, (n - 1) * each)]
+            pltpu.make_async_remote_copy(
+                src_ref=cut, dst_ref=cut, send_sem=sem.at[g], recv_sem=brecv.at[0],
+                device_id={"owner": c_dev},
+            ).wait_send()
 
 
 def fused_body(queries, probes, passages, centroids, counts):
@@ -566,31 +559,30 @@
         in_specs=[hbm] * 5,
         out_specs=(vmem, vmem),
         scratch_shapes=[
-            pltpu.VMEM((clusters // GROUP, GROUP * span + clusters, width), jnp.bfloat16),
+            pltpu.VMEM((2, clusters * span // 2 + clusters, width), jnp.bfloat16),
             pltpu.VMEM((n, per_device, width), jnp.bfloat16),
-            pltpu.VMEM((clusters, wide), jnp.float32),
             pltpu.VMEM((1, clusters), jnp.int32),
             pltpu.VMEM((probe_count, per_device), jnp.int32),
             pltpu.VMEM((n, tables + 1, 1, LANES), jnp.int32),
             pltpu.VMEM((pairs, LANES), jnp.int32),
-            pltpu.VMEM((wide, width), jnp.bfloat16),
-            pltpu.VMEM((span, wide), jnp.float32),
+            pltpu.VMEM((width, wide), jnp.bfloat16),
+            pltpu.VMEM((span // 2, wide), jnp.float32),
             pltpu.VMEM((clusters, LANES), jnp.float32),
-            pltpu.VMEM((n * cap, LANES), jnp.int32),
-            pltpu.VMEM((n // 2, 1, LANES), jnp.float32),
-            pltpu.VMEM((n * cap, LANES), jnp.int32),
-            pltpu.VMEM((n, 1, LANES), jnp.float32),
+            pltpu.VMEM((2, n * cap // 2, LANES), jnp.int32),
+            pltpu.VMEM((2, n, 1, LANES), jnp.float32),
+            pltpu.VMEM((2, n * cap // 2, LANES), jnp.int32),
+            pltpu.VMEM((2, n, 1, LANES), jnp.float32),
             pltpu.SMEM((n, 1, LANES), jnp.int32),
-            dma((clusters,)),
-            dma((3 + clusters // GROUP,)),
-            dma((n, 2, 4)),
-            dma((n, 4)),
+            dma((2,)),
+            dma((3,)),
+            dma((3,)),
+            dma((3,)),
             dma((n, 2)),
             dma((n,)),
-            dma((n,)),
-            dma((n,)),
-            dma((n,)),
-            dma((n,)),
+            dma((2,)),
+            dma((2,)),
+            dma((n // 4,)),
+            dma((n // 4,)),
         ],
         compiler_params=pltpu.CompilerParams(
             collective_id=0, has_side_effects=True, vmem_limit_bytes=48 * 2**20
@@ -612,7 +604,7 @@
     fits = (
         n == 16 and clusters % 16 == 0 and 2 * cap == LANES and n * probe_count == LANES and span == 2 * LANES
         and power_of_two(clusters) and power_of_two(per_device) and power_of_two(probe_count)
-        and clusters % GROUP == 0 and clusters <= LANES and per_device == cap
+        and clusters <= LANES and per_device == cap
         and clusters * per_device * n * cap < 2**23 and width % LANES == 0 and held < 32 * 2**20
     )
     chosen = fused_body if fits else routed_body

time: 38.2 us -> 35.8 us (0.937)
  Pallas kernels: 36.1 us -> 33.7 us
    pallas_call x1, Pallas kernels: 36.1 us -> 33.7 us  [fused_body(): pl.pallas_call(lambda *refs: owner_kernel(n, *refs), out_shape=(jax.Shape...]
where the time goes in v3:
time: 35.8 us; the launch traced here: 35.6 us
  Pallas kernels  33.7 us (94%)
  local copies, waits for them, and re-layouts  1.31 us (4%)
  between operations  0.64 us (2%)
    pallas_call x1, Pallas kernels, fused_body(): pl.pallas_call(lambda *refs: owner_kernel(n, *refs), out_shape=(jax.Shape...  33.7 us
    unnamed x2, local copies, waits for them, and re-layouts  1.31 us

profile of v3, /device:TPU:0, one launch (start us, length us, event | category | flops | bytes accessed | tf_op | source)
XLA Modules:
  0.0 35.6 jit_solution(9078764871560062319)
XLA Ops:
  0.6 33.7 %shard_map.68 = (f32[512,256]{1,0:T(8,128)S(1)}, s32[1,64]{1,0:T(1,128)S(1)}) custom-call(bf16[64,1024]{1,0:T(8,128)(2,1)} %refs_0_.1, s32[8,64]{1,0:T(8,128)} %bitcast.6, bf16[16,256,1024]{2,1,0:T(8,128)(2,1)} %refs_2_.1, bf16[16,1024]{1,0:T(8,128)(2,1)} %refs_3_.1, s32[1,16]{1,0:T(1,128)} %bitcast.7), custom_call_target="tpu_custom_call" | custom-call | tf_op jit(solution)/shard_map/pallas_call | solution.py:553
  34.3 0.8 %copy.9 = f32[64,8,256]{2,1,0:T(8,128)} copy(f32[64,8,256]{2,1,0:T(8,128)S(1)} %bitcast.4) | data formatting | bytes 1048576
  35.1 0.5 %copy.10 = s32[64]{0:T(128)} copy(s32[64]{0:T(128)S(1)} %bitcast.5) | data formatting | bytes 512

commit v4 on v3

--- a/solution.py
+++ b/solution.py
@@ -279,10 +279,10 @@
 
     def chips_of(u):
         inner = near > 0
-        first = pick_of(u, (0, 2, jnp.where(inner, 0, 3), jnp.where(inner, 3, 2)))
+        first = pick_of(u, (1, 2, jnp.where(inner, 2, 3), 3))
         first_far = pick_of(u, (0, 0, jnp.where(inner, 1, 0), jnp.where(inner, 0, 1)))
-        second = pick_of(u, (1, jnp.where(inner, 1, 0), jnp.where(inner, 2, 1), 3))
-        second_far = jnp.where(u == 0, 0, 1)
+        second = pick_of(u, (0, jnp.where(inner, 1, 0), jnp.where(inner, 0, 1), jnp.where(inner, 3, 2)))
+        second_far = pick_of(u, (0, 1, 1, 1))
 
         def chip(k, other):
             return plane_of(k) * 2 + jnp.where(other == 1, 1 - y, y)
@@ -419,14 +419,9 @@
             def _():
                 service(k, (0, 2))
 
-            @pl.when((g == 0) == (k > 0))
+            @pl.when(g == 0)
             def _():
                 service(k, (1,))
-
-            @pl.when((g == 1) & (k == 0) & (near > 0))
-            def _():
-                for h in (0, 2, 1):
-                    forward_y(planes - 1, h)
 
             return carry
 
@@ -439,7 +434,7 @@
         @pl.when(near > 0)
         def _():
             forward_z(planes - 1, h)
-            forward_c(planes - 1, h)
+            forward_plane(planes - 1, h)
 
         relay_y(0, h)
 
@@ -537,6 +532,17 @@
                 src_ref=cut, dst_ref=cut, send_sem=sem.at[g], recv_sem=brecv.at[0],
                 device_id={"owner": c_dev},
             ).wait_send()
+
+
+def deliver(scores_ref, visits_ref, scores_out, visits_out, sem):
+    copies = (
+        pltpu.make_async_copy(scores_ref, scores_out, sem.at[0]),
+        pltpu.make_async_copy(visits_ref, visits_out, sem.at[1]),
+    )
+    for copy in copies:
+        copy.start()
+    for copy in copies:
+        copy.wait()
 
 
 def fused_body(queries, probes, passages, centroids, counts):
@@ -588,6 +594,17 @@
             collective_id=0, has_side_effects=True, vmem_limit_bytes=48 * 2**20
         ),
     )(*[pltpu.with_memory_space_constraint(v, pltpu.HBM) for v in (queries, probes.T, passages, centroids, counts.reshape(1, clusters))])
+    scores, visits = pl.pallas_call(
+        deliver,
+        out_shape=(
+            jax.ShapeDtypeStruct((pairs, span), jnp.float32),
+            jax.ShapeDtypeStruct((1, per_device), jnp.int32),
+        ),
+        in_specs=[vmem] * 2,
+        out_specs=(pl.BlockSpec(memory_space=pl.ANY), pl.BlockSpec(memory_space=pl.ANY)),
+        scratch_shapes=[dma((2,))],
+        compiler_params=pltpu.CompilerParams(vmem_limit_bytes=2**20),
+    )(*[pltpu.with_memory_space_constraint(v, pltpu.VMEM) for v in (scores, visits)])
     return scores.reshape(per_device, probe_count, span), visits.reshape(per_device)
 
 

time: 35.8 us -> 34.5 us (0.964)
  local copies, waits for them, and re-layouts: 1.31 us -> 0 us
    unnamed x2 -> x0, local copies, waits for them, and re-layouts: 1.31 us -> none
    pallas_call x0 -> x1, Pallas kernels: none -> 0.81 us  [fused_body(): pl.pallas_call(deliver, out_shape=(jax.ShapeDtypeStruct((pairs, span), jn...]
    pallas_call x1, Pallas kernels: 33.7 us -> 32.9 us  [fused_body(): pl.pallas_call(lambda *refs: owner_kernel(n, *refs), out_shape=(jax.Shape...]
where the time goes in v4:
time: 34.5 us; the launch traced here: 34.4 us
  Pallas kernels  33.7 us (98%)
  between operations  0.64 us (2%)
    pallas_call x1, Pallas kernels, fused_body(): pl.pallas_call(lambda *refs: owner_kernel(n, *refs), out_shape=(jax.Shape...  32.9 us
    pallas_call x1, Pallas kernels, fused_body(): pl.pallas_call(deliver, out_shape=(jax.ShapeDtypeStruct((pairs, span), jn...  0.81 us

profile of v4, /device:TPU:0, one launch (start us, length us, event | category | flops | bytes accessed | tf_op | source)
XLA Modules:
  0.0 34.4 jit_solution(4649954027461811497)
XLA Ops:
  0.6 32.9 %shard_map.68 = (f32[512,256]{1,0:T(8,128)S(1)}, s32[1,64]{1,0:T(1,128)S(1)}) custom-call(bf16[64,1024]{1,0:T(8,128)(2,1)} %refs_0_.1, s32[8,64]{1,0:T(8,128)} %bitcast.4, bf16[16,256,1024]{2,1,0:T(8,128)(2,1)} %refs_2_.1, bf16[16,1024]{1,0:T(8,128)(2,1)} %refs_3_.1, s32[1,16]{1,0:T(1,128)} %bitcast.5), custom_call_target="tpu_custom_call" | custom-call | tf_op jit(solution)/shard_map/pallas_call | solution.py:559
  33.5 0.8 %shard_map.69 = (f32[512,256]{1,0:T(8,128)}, s32[1,64]{1,0:T(1,128)}) custom-call(f32[512,256]{1,0:T(8,128)S(1)} %get-tuple-element.6.scores_ref, s32[1,64]{1,0:T(1,128)S(1)} %get-tuple-element.7.visits_ref), custom_call_target="tpu_custom_call" | custom-call | tf_op jit(solution)/shard_map/pallas_call | solution.py:597

commit v5 on v4

--- a/solution.py
+++ b/solution.py
@@ -171,11 +171,14 @@
     def push(s, h, target, dev):
         chunk(s, h, target, dev).start()
 
-    def drain(way, blocks):
-        for ref, sem in ((qs, qsend), (ms, msend)):
+    def drain(way, blocks, halves):
+        for cut, sem in (
+            (pass_v.at[0, pl.ds(0, halves * piece)], qsend),
+            (ms.at[pl.ds(0, blocks)], msend),
+        ):
             pltpu.make_async_remote_copy(
-                src_ref=ref.at[pl.ds(0, blocks)], dst_ref=ref.at[pl.ds(0, blocks)],
-                send_sem=sem.at[way], recv_sem=mrecv.at[0], device_id={"owner": c_dev},
+                src_ref=cut, dst_ref=cut, send_sem=sem.at[way], recv_sem=mrecv.at[0],
+                device_id={"owner": c_dev},
             ).wait_send()
 
     def arrive(s, h):
@@ -263,13 +266,17 @@
 
     far = planes - 1 - near
 
+    inner = near > 0
+    low_side = z < planes - 1 - z
+
     def plane_of(k):
-        return z + long_side * jnp.where(k <= far, k, far - k)
+        at = jnp.where(inner & low_side & (k % 2 == 1), planes - k, k)
+        return z + long_side * jnp.where(at <= far, at, far - at)
 
     def collect_of(k):
-        ends = jnp.where(k == 1, 2, jnp.where(k == 2, 1, k))
-        inner = jnp.where(k == 1, -1, jnp.where(k > 1, k - 1, 0))
-        return z + long_side * jnp.where(near == 0, ends, inner)
+        ends = jnp.where(low_side | (k == 0) | (k == 3), k, 3 - k)
+        middle = jnp.where(k == 0, 0, jnp.where(k == 1, -1, jnp.where(low_side, k - 1, 4 - k)))
+        return z + long_side * jnp.where(inner, middle, ends)
 
     def pick_of(u, values):
         found = values[0]
@@ -319,13 +326,25 @@
         s = plane_of(k) * 4 + (1 - y) * 2 + c
         arrive(s, h)
         push(s, h, 3, c_dev)
+        if h == 1:
+            @pl.when(inner & (k == 2) & low_side)
+            def _():
+                push(s, h, 0, me - 4)
+
+            @pl.when(inner & (k == 2) & jnp.logical_not(low_side))
+            def _():
+                push(s, h, 1, me + 4)
 
     def service(u, pieces):
         for h in pieces:
             @pl.when(u + 2 <= far)
             def _():
                 forward_z(u + 2, h)
-                forward_plane(u + 2, h)
+                forward_c(u + 2, h)
+
+                @pl.when(inner | (u + 2 < 3) | (h != 1))
+                def _():
+                    forward_y(u + 2, h)
 
             @pl.when(u + 1 < planes)
             def _():
@@ -415,26 +434,23 @@
                     for copy in back_pair(g, s):
                         copy.start()
 
-            @pl.when(g == 0)
+            @pl.when((g == 0) == ((k != 2) | (near > 0)))
             def _():
-                service(k, (0, 2))
-
-            @pl.when(g == 0)
-            def _():
-                service(k, (1,))
+                service(k, (0, 2, 1))
 
             return carry
 
         lax.fori_loop(0, 2, one_half, 0)
 
+    lead_k = jnp.where(inner & low_side, planes - 1, 1)
     for h in (0, 2, 1):
-        forward_z(1, h)
-        forward_plane(1, h)
-
-        @pl.when(near > 0)
-        def _():
-            forward_z(planes - 1, h)
-            forward_plane(planes - 1, h)
+        forward_z(lead_k, h)
+        forward_plane(lead_k, h)
+
+        @pl.when(inner)
+        def _():
+            forward_z(planes - lead_k, h)
+            forward_plane(planes - lead_k, h)
 
         relay_y(0, h)
 
@@ -515,16 +531,17 @@
 
     lax.fori_loop(0, planes, collect, 0)
 
-    @pl.when(near > 0)
+    @pl.when(inner)
     def _():
-        drain(0, planes + 1)
-
-    @pl.when(near == 0)
+        drain(0, planes + 1, 2 * planes + 3)
+        drain(1, planes, 2 * planes)
+
+    @pl.when(jnp.logical_not(inner))
     def _():
-        drain(0, 1)
-
-    drain(1, planes)
-    drain(2, 2 * planes)
+        drain(0, 1, 2)
+        drain(1, planes, 2 * planes - 1)
+
+    drain(2, 2 * planes, 4 * planes)
     for g in range(2):
         for ref, sem, each in ((sendb, bsend, short), (sends, ssend, 1)):
             cut = ref.at[g, pl.ds(0, (n - 1) * each)]

time: 34.5 us -> 34 us (0.986)
  Pallas kernels: 33.7 us -> 33.2 us
    pallas_call x1, Pallas kernels: 32.9 us -> 32.4 us  [fused_body(): pl.pallas_call(lambda *refs: owner_kernel(n, *refs), out_shape=(jax.Shape...]
where the time goes in v5:
time: 34 us; the launch traced here: 33.9 us
  Pallas kernels  33.2 us (98%)
  between operations  0.64 us (2%)
    pallas_call x1, Pallas kernels, fused_body(): pl.pallas_call(lambda *refs: owner_kernel(n, *refs), out_shape=(jax.Shape...  32.4 us
    pallas_call x1, Pallas kernels, fused_body(): pl.pallas_call(deliver, out_shape=(jax.ShapeDtypeStruct((pairs, span), jn...  0.81 us

profile of v5, /device:TPU:0, one launch (start us, length us, event | category | flops | bytes accessed | tf_op | source)
XLA Modules:
  0.0 33.9 jit_solution(17229366045328325510)
XLA Ops:
  0.6 32.4 %shard_map.68 = (f32[512,256]{1,0:T(8,128)S(1)}, s32[1,64]{1,0:T(1,128)S(1)}) custom-call(bf16[64,1024]{1,0:T(8,128)(2,1)} %refs_0_.1, s32[8,64]{1,0:T(8,128)} %bitcast.4, bf16[16,256,1024]{2,1,0:T(8,128)(2,1)} %refs_2_.1, bf16[16,1024]{1,0:T(8,128)(2,1)} %refs_3_.1, s32[1,16]{1,0:T(1,128)} %bitcast.5), custom_call_target="tpu_custom_call" | custom-call | tf_op jit(solution)/shard_map/pallas_call | solution.py:576
  33.0 0.8 %shard_map.69 = (f32[512,256]{1,0:T(8,128)}, s32[1,64]{1,0:T(1,128)}) custom-call(f32[512,256]{1,0:T(8,128)S(1)} %get-tuple-element.6.scores_ref, s32[1,64]{1,0:T(1,128)S(1)} %get-tuple-element.7.visits_ref), custom_call_target="tpu_custom_call" | custom-call | tf_op jit(solution)/shard_map/pallas_call | solution.py:614

commit v6 on v5

--- a/solution.py
+++ b/solution.py
@@ -165,7 +165,7 @@
         cut = pl.ds(h * piece, piece)
         return pltpu.make_async_remote_copy(
             src_ref=qs.at[s, cut], dst_ref=qs.at[s, cut],
-            send_sem=qsend.at[max(target - 1, 0)], recv_sem=qrecv.at[s, h], device_id={"owner": dev},
+            send_sem=qsend.at[max(target - 1, 0)], recv_sem=qrecv.at[n + s // 2 if target == 3 else s // 2 * 2 + h], device_id={"owner": dev},
         )
 
     def push(s, h, target, dev):
@@ -458,8 +458,12 @@
 
     def step(k, carry):
         for chip in chips_of(k):
-            for h in range(3):
-                arrive(2 * chip + (1 - c), h)
+            s = 2 * chip + (1 - c)
+            pltpu.make_async_remote_copy(
+                src_ref=qs.at[s], dst_ref=qs.at[s], send_sem=qsend.at[2],
+                recv_sem=qrecv.at[n + s // 2], device_id={"owner": c_dev},
+            ).wait_recv()
+            arrive(s, 2)
 
         @pl.when(k == planes - 1)
         def _():
@@ -600,7 +604,7 @@
             dma((3,)),
             dma((3,)),
             dma((3,)),
-            dma((n, 2)),
+            dma((n + n // 2,)),
             dma((n,)),
             dma((2,)),
             dma((2,)),

time: 34 us -> 34 us (level)
  no operation moved by 1% of the time
where the time goes in v6:
time: 34 us; the launch traced here: 33.9 us
  Pallas kernels  33.2 us (98%)
  between operations  0.64 us (2%)
    pallas_call x1, Pallas kernels, fused_body(): pl.pallas_call(lambda *refs: owner_kernel(n, *refs), out_shape=(jax.Shape...  32.4 us
    pallas_call x1, Pallas kernels, fused_body(): pl.pallas_call(deliver, out_shape=(jax.ShapeDtypeStruct((pairs, span), jn...  0.81 us

profile of v6, /device:TPU:0, one launch (start us, length us, event | category | flops | bytes accessed | tf_op | source)
XLA Modules:
  0.0 33.9 jit_solution(16957404367862752949)
XLA Ops:
  0.6 32.4 %shard_map.68 = (f32[512,256]{1,0:T(8,128)S(1)}, s32[1,64]{1,0:T(1,128)S(1)}) custom-call(bf16[64,1024]{1,0:T(8,128)(2,1)} %refs_0_.1, s32[8,64]{1,0:T(8,128)} %bitcast.4, bf16[16,256,1024]{2,1,0:T(8,128)(2,1)} %refs_2_.1, bf16[16,1024]{1,0:T(8,128)(2,1)} %refs_3_.1, s32[1,16]{1,0:T(1,128)} %bitcast.5), custom_call_target="tpu_custom_call" | custom-call | tf_op jit(solution)/shard_map/pallas_call | solution.py:580
  33.0 0.8 %shard_map.69 = (f32[512,256]{1,0:T(8,128)}, s32[1,64]{1,0:T(1,128)}) custom-call(f32[512,256]{1,0:T(8,128)S(1)} %get-tuple-element.6.scores_ref, s32[1,64]{1,0:T(1,128)S(1)} %get-tuple-element.7.visits_ref), custom_call_target="tpu_custom_call" | custom-call | tf_op jit(solution)/shard_map/pallas_call | solution.py:618
